TPU v7x, 128 devices: a whole 4x4x4 slice. The times are simulated.
128 devices in a mesh: px: 8 (over z_hi, y), py: 16 (over x, z_lo, core).
Axes of the slice: x: 4, y: 4, z: 4 (z_hi: 2, z_lo: 2; z = z_hi * 2 + z_lo), core: 2. Of those that a mesh axis runs over, the one named last changes fastest.
Arguments:
- white_noise: float32 [2, 128, 512, 256], P(None, 'px', 'py'), may hold values from -6 to 6
- spectrum: float32 [128, 512, 256], P('px', 'py'), may hold values from 0.1 to 2, as said below
- group_table: int32 [3, 16], replicated, may hold values from 0 to 15, each once within a row
Outputs:
- modulus: float32 [2, 128, 512, 256], P(None, 'px', 'py')
- level_one: float32 [2, 64, 256, 128], P(None, 'px', 'py')
- level_two: float32 [2, 32, 128, 64], P(None, 'px', 'py')
- level_three: float32 [2, 16, 64, 32], P(None, 'px', 'py')
Inputs may be any that keep to these rules, and one draw needn't show every extreme that they name: spectrum[j, m, k] equals spectrum[(128 - j) % 128, (512 - m) % 512, (256 - k) % 256]. `group_table`: each row is a permutation of 0 to 15.
All inputs are finite; a program needn't handle non-finite values.
Results may differ from a plain program's by a relative error of at most 0.000088.
Values sent between devices are 32-bit elements; how exact they have to be, the bound alone decides.
A program may use at most 192 MiB of HBM per device.

v0:
```python
import numpy as np

import jax
import jax.numpy as jnp
from jax import lax
from jax.experimental import pallas as pl
from jax.experimental.pallas import tpu as pltpu
from jax.sharding import PartitionSpec as P


def angles_of(length):
    positions = np.arange(length, dtype=np.int64)
    return (positions[:, None] * positions[None, :] % length) * (2.0 * np.pi / length)


def complex_array(length, direction):
    angles = angles_of(length)
    cos, sin = np.cos(angles), direction * np.sin(angles)
    return np.stack([np.stack([cos, sin], 1), np.stack([-sin, cos], 1)], 0)


def complex_table(length, direction):
    return jnp.asarray(complex_array(length, direction), jnp.float32)


def half_tables(length):
    angles = angles_of(length)[:, : length // 2]
    ahead = np.stack([np.cos(angles), -np.sin(angles)], 1)
    back = 2.0 * ahead
    nyquist = np.where(np.arange(length) % 2 == 0, 1.0, -1.0)
    ahead[:, 1, 0] = nyquist
    back[:, 0, 0] = 1.0
    back[:, 1, 0] = nyquist
    return jnp.asarray(ahead, jnp.float32), jnp.asarray(back, jnp.float32)


def einsum(pattern, left, right):
    return jnp.einsum(pattern, left, right, precision=lax.Precision.HIGH)


def swap_first(values):
    first = values[:, :, :1]
    turned = jnp.swapaxes(first, 0, 1)
    return jnp.concatenate([turned, values[:, :, 1:]], 2)


def coarsen(values):
    members, size_x, size_y, size_z = values.shape
    blocks = values.reshape(members, size_x // 2, 2, size_y // 2, 2, size_z // 2, 2)
    return blocks.mean(axis=(2, 4, 6))


def general_path(white_noise, spectrum, group_table):
    members, cells_x, cells_y, length_z = white_noise.shape
    size_px, size_py = lax.axis_size("px"), lax.axis_size("py")
    length_x, length_y = cells_x * size_px, cells_y * size_py
    half_z = length_z // 2
    block_py, block = half_z // size_py, half_z // size_py // size_px
    z_ahead, z_back = half_tables(length_z)
    scale = 1.0 / (length_x * length_y * length_z)

    table = jnp.transpose(spectrum, (2, 0, 1))
    last = jnp.broadcast_to(table[half_z : half_z + 1], (size_py, 1, cells_x, cells_y))
    table = jnp.concatenate([table[:half_z].reshape(size_py, block_py, cells_x, cells_y), last], 1)
    table = lax.all_to_all(table, "py", split_axis=0, concat_axis=3, tiled=True)[0]
    last = jnp.broadcast_to(table[block_py:], (size_px, 1, cells_x, length_y))
    table = jnp.concatenate([table[:block_py].reshape(size_px, block, cells_x, length_y), last], 1)
    table = lax.all_to_all(table, "px", split_axis=0, concat_axis=2, tiled=True)[0] * scale
    is_first = (lax.axis_index("px") == 0) & (lax.axis_index("py") == 0)
    other = jnp.where(is_first, table[block:], table[:1])
    tables = jnp.stack([table[:block], jnp.concatenate([other, table[1:block]], 0)], 0)

    values = einsum("fxyz,zck->fckxy", white_noise, z_ahead)
    values = swap_first(values)
    values = lax.all_to_all(values, "py", split_axis=2, concat_axis=4, tiled=True)
    values = einsum("fckxy,cydm->fdkxm", values, complex_table(length_y, -1.0))
    values = lax.all_to_all(values, "px", split_axis=2, concat_axis=3, tiled=True)
    values = einsum("fckxm,cxdj->fdkjm", values, complex_table(length_x, -1.0))
    values = values * tables[:, None]
    values = einsum("fckjm,cjdx->fdkxm", values, complex_table(length_x, 1.0))
    values = lax.all_to_all(values, "px", split_axis=3, concat_axis=2, tiled=True)
    values = einsum("fckxm,cmdy->fdkxy", values, complex_table(length_y, 1.0))
    values = lax.all_to_all(values, "py", split_axis=4, concat_axis=2, tiled=True)
    values = swap_first(values)
    fields = einsum("fckxy,zck->fxyz", values, z_back)
    modulus = jnp.exp(0.5 * fields)

    levels = []
    level = modulus
    for _ in range(3):
        level = coarsen(level)
        levels.append(level)
    pieces = [jnp.reshape(level, (size_py, -1)) for level in levels]
    widths = [piece.shape[1] for piece in pieces]
    joined = jnp.concatenate(pieces, 1)
    spread = lax.all_to_all(joined, "py", split_axis=0, concat_axis=0, tiled=True)
    picked, start = [], 0
    for index, width in enumerate(widths):
        part = spread[:, start : start + width]
        picked.append(jnp.take(part, group_table[index], axis=0))
        start += width
    joined = lax.all_to_all(
        jnp.concatenate(picked, 1), "py", split_axis=0, concat_axis=0, tiled=True
    )
    routed, start = [], 0
    for level, width in zip(levels, widths):
        routed.append(joined[:, start : start + width].reshape(level.shape))
        start += width
    return (modulus, routed[0], routed[1], routed[2])


LANES = 128
MESH = pl.DeviceIdType.MESH


def dot(left, right):
    return jnp.dot(
        left, right, precision=lax.Precision.HIGHEST, preferred_element_type=jnp.float32
    )


def lane_of(shape):
    return lax.broadcasted_iota(jnp.int32, shape, len(shape) - 1)


def exchange(arrays, width):
    arrays = list(arrays)
    lane = lane_of(arrays[0].shape)
    distance = 1
    while distance < len(arrays):
        step = distance * width
        low = (lane // step) % 2 == 0
        for index in range(len(arrays)):
            if (index // distance) % 2 == 0:
                first, second = arrays[index], arrays[index + distance]
                arrays[index] = jnp.where(low, first, pltpu.roll(second, step, 1))
                arrays[index + distance] = jnp.where(
                    low, pltpu.roll(first, LANES - step, 1), second
                )
        distance *= 2
    return arrays


def swap_slot(first, second):
    at_zero = lane_of(first.shape) == 0
    return jnp.where(at_zero, second, first), jnp.where(at_zero, first, second)


def z_forward_kernel(sizes, noise_ref, spectrum_ref, table_ref, out_ref, held):
    lo, hi, kept = sizes
    cells_y = noise_ref.shape[2]
    for f in range(2):
        rows = noise_ref[f].reshape(lo * hi * cells_y, noise_ref.shape[3])
        held[f] = dot(rows, table_ref[...])

    def tile(f, c, x):
        return held[f, pl.ds(x * cells_y, cells_y), pl.ds(c * LANES, LANES)]

    for xh in range(hi):
        tiles = {}
        for xl in range(lo):
            x = xh * lo + xl
            mixed = swap_slot(tile(0, 1, x), tile(1, 0, x))
            members = ((tile(0, 0, x), mixed[0]), (mixed[1], tile(1, 1, x)))
            for f in range(2):
                for c in range(2):
                    tiles[f, c, xl] = members[f][c]
        for f in range(2):
            for c in range(2):
                moved = exchange([tiles[f, c, xl] for xl in range(lo)], kept)
                for p in range(lo):
                    out_ref[p, (f * 2 + c) * hi + xh] = moved[p]
    group = lane_of((cells_y, LANES))
    last = jnp.zeros((cells_y, LANES), jnp.float32)
    for xh in range(hi):
        names = [xh * lo + xl for xl in range(lo)]
        moved = exchange([spectrum_ref[x, :, pl.ds(0, LANES)] for x in names], kept)
        for p in range(lo):
            out_ref[p, 4 * hi + xh] = moved[p]
        for xl in range(lo):
            value = spectrum_ref[names[xl], :, pl.ds(LANES, 1)]
            last = jnp.where(group == xl * kept + xh, value, last)
    for p in range(lo):
        out_ref[p, 5 * hi] = last


def y_forward_kernel(sizes, in_ref, table_ref, out_ref):
    lo, hi, kept = sizes
    length_y = table_ref.shape[1]
    ranks = 2 * hi
    half = length_y // 2

    def whole(t):
        return in_ref[:, t].reshape(length_y, LANES)

    for f in range(2):
        arrays = [None] * ranks
        for xh in range(hi):
            pair = [whole((f * 2 + c) * hi + xh) for c in range(2)]
            product = dot(table_ref[...], jnp.concatenate(pair, 1))
            by_cos, by_sin = product[:length_y], product[length_y:]
            arrays[xh] = by_cos[:, :LANES] + by_sin[:, LANES:]
            arrays[hi + xh] = by_cos[:, LANES:] - by_sin[:, :LANES]
        moved = exchange(arrays, kept // ranks)
        for r in range(ranks):
            out_ref[r, pl.ds(f * length_y, length_y)] = moved[r]
    halves = []
    for mh in range(2):
        for xh in range(hi):
            halves.append(whole(4 * hi + xh)[mh * half : (mh + 1) * half])
    moved = exchange(halves, kept // ranks)
    last = whole(5 * hi)
    packed = last[:half] + pltpu.roll(last[half:], hi, 1)
    for r in range(ranks):
        out_ref[r, pl.ds(2 * length_y, half)] = moved[r]
        out_ref[r, pl.ds(2 * length_y + half, half)] = packed


def x_kernel(sizes, first_ref, in_ref, ahead_ref, back_ref, out_ref):
    lo, hi, kept = sizes
    ranks = 2 * hi
    length_y = out_ref.shape[1] // 2
    half = length_y // 2
    lane = lane_of((half, LANES))
    low = (lane // (hi * ranks)) % 2 == 0
    parts = [in_ref[r, pl.ds(2 * length_y, half)] for r in range(ranks)]
    tables = []
    for part in exchange(parts, 1):
        upper = jnp.where(low, part, pltpu.roll(part, hi * ranks, 1))
        lower = jnp.where(low, pltpu.roll(part, LANES - hi * ranks, 1), part)
        tables.append(jnp.concatenate([upper, lower], 0))
    last = [in_ref[r, pl.ds(2 * length_y + half, half)] for r in range(ranks)]
    last = jnp.concatenate(last, 1)
    source = lax.broadcasted_iota(jnp.int32, (ranks * LANES, LANES), 0)
    target = lax.broadcasted_iota(jnp.int32, (ranks * LANES, LANES), 1)
    same = (source // LANES == target % ranks) & ((source % LANES) // kept == target // kept)
    level = (target // ranks) % hi
    picked = []
    for mh in range(2):
        chosen = same & (source % kept == mh * hi + level)
        picked.append(dot(last, chosen.astype(jnp.float32)))
    last = jnp.concatenate(picked, 0)
    is_first = lax.broadcasted_iota(jnp.int32, last.shape, 0) * 0 + first_ref[0] == 1
    other = jnp.where(is_first, last, tables[0])
    for f in range(2):
        rows = pl.ds(f * length_y, length_y)
        arrays = exchange([in_ref[r, rows] for r in range(ranks)], 1)
        for q in range(ranks):
            table = other if f == 1 and q == 0 else tables[q]
            arrays[q] = dot(dot(arrays[q], ahead_ref[...]) * table, back_ref[...])
        arrays = exchange(arrays, 1)
        for r in range(ranks):
            out_ref[r, rows] = arrays[r]


def y_back_kernel(sizes, in_ref, table_ref, out_ref):
    lo, hi, kept = sizes
    ranks = 2 * hi
    length_y = table_ref.shape[1]
    cells_y = length_y // lo
    for f in range(2):
        rows = pl.ds(f * length_y, length_y)
        arrays = exchange([in_ref[r, rows] for r in range(ranks)], kept // ranks)
        for xh in range(hi):
            product = dot(table_ref[...], jnp.concatenate([arrays[xh], arrays[hi + xh]], 1))
            by_cos, by_sin = product[:length_y], product[length_y:]
            real = by_cos[:, :LANES] - by_sin[:, LANES:]
            imag = by_cos[:, LANES:] + by_sin[:, :LANES]
            out_ref[:, (f * 2) * hi + xh] = real.reshape(lo, cells_y, LANES)
            out_ref[:, (f * 2 + 1) * hi + xh] = imag.reshape(lo, cells_y, LANES)


def pool_matrix(rows, columns, weight, transposed):
    long_axis = 0 if transposed else 1
    shape = (columns, rows) if transposed else (rows, columns)
    long = lax.broadcasted_iota(jnp.int32, shape, long_axis)
    short = lax.broadcasted_iota(jnp.int32, shape, 1 - long_axis)
    return jnp.where(long // 2 == short, weight, 0.0).astype(jnp.float32)


def pool_rows(cells_x, cells_y):
    shape = (cells_x * cells_y // 4, cells_x * cells_y)
    short = lax.broadcasted_iota(jnp.int32, shape, 0)
    long = lax.broadcasted_iota(jnp.int32, shape, 1)
    same_x = long // (2 * cells_y) == short // (cells_y // 2)
    same_y = (long % cells_y) // 2 == short % (cells_y // 2)
    return jnp.where(same_x & same_y, 0.125, 0.0).astype(jnp.float32)


def z_back_kernel(sizes, in_ref, table_ref, modulus_ref, coarse_ref, held):
    lo, hi, kept = sizes
    cells_y = in_ref.shape[2]
    cells_x = lo * hi
    length_z = table_ref.shape[0]
    for xh in range(hi):
        tiles = {}
        for f in range(2):
            for c in range(2):
                arrays = [in_ref[p, (f * 2 + c) * hi + xh] for p in range(lo)]
                tiles[f, c] = exchange(arrays, kept)
        for xl in range(lo):
            mixed = swap_slot(tiles[0, 1][xl], tiles[1, 0][xl])
            members = ((tiles[0, 0][xl], mixed[0]), (mixed[1], tiles[1, 1][xl]))
            rows = pl.ds((xh * lo + xl) * cells_y, cells_y)
            for f in range(2):
                for c in range(2):
                    held[f, rows, pl.ds(c * LANES, LANES)] = members[f][c]
    coarse_ref[...] = jnp.zeros(coarse_ref.shape, jnp.float32)
    for f in range(2):
        values = jnp.exp(0.5 * dot(held[f], table_ref[...]))
        modulus_ref[f] = values.reshape(cells_x, cells_y, length_z)
        size_x, size_y, size_z = cells_x, cells_y, length_z
        start = 0
        for _ in range(3):
            right = pool_matrix(size_z // 2, size_z, 1.0, True)
            values = dot(pool_rows(size_x, size_y), dot(values, right))
            size_x, size_y, size_z = size_x // 2, size_y // 2, size_z // 2
            height = 2 * size_x * size_y // lo
            for d in range(lo // 2):
                piece = values[d * height : (d + 1) * height]
                place = (f * lo // 2 + d, pl.ds(start, height), pl.ds(0, size_z))
                coarse_ref[place] = piece
            start += height


def pick_kernel(heights, table_ref, in_ref, out_ref):
    for column in range(in_ref.shape[0]):
        start = 0
        for index, height in enumerate(heights):
            rows = pl.ds(start, height)
            out_ref[column, rows] = in_ref[table_ref[index, column], rows]
            start += height


def spread_kernel(axis, tail, used, in_ref, out_ref, own_sem, sends, recvs, tail_sends, tail_recvs):
    count, height = in_ref.shape[0], in_ref.shape[1]
    me = lax.axis_index(axis)
    used = used()
    rest = pl.ds(tail, height - tail)
    barrier = pltpu.get_barrier_semaphore()
    for away in range(1, count):
        peer = lax.rem(me + away, count)
        pl.semaphore_signal(barrier, inc=1, device_id={axis: peer}, device_id_type=MESH)
    own = pltpu.make_async_copy(in_ref.at[me], out_ref.at[me], own_sem)
    own.start()
    pl.semaphore_wait(barrier, count - 1)
    copies, extras = [], []
    for away in range(1, count):
        peer = lax.rem(me + away, count)
        copy = pltpu.make_async_remote_copy(
            src_ref=in_ref.at[peer, pl.ds(0, tail)],
            dst_ref=out_ref.at[me, pl.ds(0, tail)],
            send_sem=sends.at[away],
            recv_sem=recvs.at[away],
            device_id={axis: peer},
            device_id_type=MESH,
        )
        copy.start()
        copies.append(copy)
    for source in range(1, count):
        extra = pltpu.make_async_remote_copy(
            src_ref=in_ref.at[0, rest],
            dst_ref=out_ref.at[source, rest],
            send_sem=tail_sends.at[source],
            recv_sem=tail_recvs.at[source],
            device_id={axis: 0},
            device_id_type=MESH,
        )
        pl.when((me == source) & used)(extra.start)
        extras.append(extra)
    for source in range(count):

        @pl.when((me != source) & jnp.logical_not((me == 0) & used))
        def _():
            out_ref[source, rest] = jnp.zeros(out_ref.shape[1:], jnp.float32)[tail:]

    own.wait()
    for copy in copies:
        copy.wait()
    for source in range(1, count):
        pl.when((me == source) & used)(extras[source - 1].wait_send)
        pl.when((me == 0) & used)(extras[source - 1].wait_recv)


def spread_call(values, axis, number, tail, used):
    count = values.shape[0]

    def body(*refs):
        spread_kernel(axis, tail, used, *refs)

    return pl.pallas_call(
        body,
        out_shape=jax.ShapeDtypeStruct(values.shape, values.dtype),
        in_specs=[pl.BlockSpec(memory_space=pltpu.VMEM)],
        out_specs=pl.BlockSpec(memory_space=pltpu.VMEM),
        scratch_shapes=[pltpu.SemaphoreType.DMA] + [pltpu.SemaphoreType.DMA((count,))] * 4,
        compiler_params=pltpu.CompilerParams(collective_id=number, has_side_effects=True),
    )(values)


def spread(values, axis):
    return lax.all_to_all(values, axis, split_axis=0, concat_axis=0, tiled=True)


def lanes_path(white_noise, spectrum, group_table):
    members, cells_x, cells_y, length_z = white_noise.shape
    size_px, size_py = lax.axis_size("px"), lax.axis_size("py")
    length_x, length_y = cells_x * size_px, cells_y * size_py
    lo, hi = size_py, cells_x // size_py
    kept = LANES // size_py
    sizes = (lo, hi, kept)
    f32 = jnp.float32
    params = pltpu.CompilerParams(vmem_limit_bytes=48 * 1024 * 1024)

    def call(body, shapes, *operands, scratch=(), scalars=0):
        out = [jax.ShapeDtypeStruct(shape, f32) for shape in shapes]
        specs = [pl.BlockSpec(memory_space=pltpu.SMEM)] * scalars
        specs += [pl.BlockSpec(memory_space=pltpu.VMEM)] * (len(operands) - scalars)
        return pl.pallas_call(
            body,
            out_shape=out,
            in_specs=specs,
            out_specs=[pl.BlockSpec(memory_space=pltpu.VMEM)] * len(out),
            scratch_shapes=list(scratch),
            compiler_params=params,
        )(*operands)

    z_ahead, z_back = half_tables(length_z)
    z_ahead = z_ahead.reshape(length_z, length_z)
    z_back = z_back.reshape(length_z, length_z).T * (1.0 / (length_x * length_y * length_z))
    angles = angles_of(length_y)
    y_table = jnp.asarray(np.concatenate([np.cos(angles), np.sin(angles)], 0), f32)
    lane = np.arange(LANES)
    part = (lane // (hi * size_px)) % 2
    place = (lane % size_px) * cells_x + (lane // size_px % hi) * lo + lane // kept

    def x_table(direction):
        table = complex_array(length_x, direction)
        rows = table[part, place]
        return jnp.asarray(rows[:, part, place], f32)

    first = (lax.axis_index("px") == 0) & (lax.axis_index("py") == 0)
    first = first.astype(jnp.int32).reshape(1)
    held = pltpu.VMEM((members, cells_x * cells_y, length_z), f32)

    def bind(body):
        def bound(*refs):
            body(sizes, *refs)

        return bound

    tiles = 4 * hi
    (values,) = call(
        bind(z_forward_kernel),
        [(size_py, tiles + hi + 1, cells_y, LANES)],
        white_noise,
        spectrum,
        z_ahead,
        scratch=[held],
    )
    values = spread_call(values, "py", 0, tiles + hi, lambda: True)
    (values,) = call(
        bind(y_forward_kernel), [(size_px, 3 * length_y, LANES)], values, y_table
    )
    values = spread_call(
        values, "px", 1, 2 * length_y + length_y // 2, lambda: lax.axis_index("py") == 0
    )
    (values,) = call(
        bind(x_kernel),
        [(size_px, 2 * length_y, LANES)],
        first,
        values,
        x_table(-1.0),
        x_table(1.0),
        scalars=1,
    )
    values = spread(values, "px")
    (values,) = call(
        bind(y_back_kernel), [(size_py, tiles, cells_y, LANES)], values, y_table
    )
    values = spread(values, "py")
    shapes = []
    heights = []
    size = (cells_x, cells_y, length_z)
    for _ in range(3):
        size = tuple(extent // 2 for extent in size)
        shapes.append((members,) + size)
        heights.append(members * size[0] * size[1] // size_py)
    modulus, coarse = call(
        bind(z_back_kernel),
        [white_noise.shape, (size_py, sum(heights), LANES)],
        values,
        z_back,
        scratch=[held],
    )
    coarse = spread(coarse, "py")

    def pick(*refs):
        pick_kernel(heights, *refs)

    (coarse,) = call(pick, [coarse.shape], group_table, coarse, scalars=1)
    coarse = spread(coarse, "py")
    routed, start = [], 0
    for shape, height in zip(shapes, heights):
        routed.append(coarse[:, start : start + height, : shape[3]].reshape(shape))
        start += height
    return (modulus, routed[0], routed[1], routed[2])


def on_device(white_noise, spectrum, group_table):
    members, cells_x, cells_y, length_z = white_noise.shape
    size_px, size_py = lax.axis_size("px"), lax.axis_size("py")
    fits = members == 2 and length_z == 2 * LANES and 2 * cells_x * size_px == LANES
    fits = fits and cells_x * 2 == size_px * size_py
    fits = fits and size_px * size_px * size_py == LANES
    chosen = lanes_path if fits else general_path
    return chosen(white_noise, spectrum, group_table)


def solution(mesh):
    in_specs = (P(None, "px", "py", None), P("px", "py", None), P())
    out_specs = (P(None, "px", "py", None),) * 4
    return jax.shard_map(
        on_device, mesh=mesh, in_specs=in_specs, out_specs=out_specs, check_vma=False
    )
```

profile of v0, /device:TPU:1, one launch (start us, length us, event | category | flops | bytes accessed | tf_op | source)
XLA Modules:
  0.0 344.1 jit_solution(2877478495509766945)
XLA Ops:
  0.7 2.4 copy.61
  4.5 7.2 %all-to-all-start.2 = ((f32[16,1,4608]{2,1,0:T(1,128)}), f32[16,1,4608]{2,1,0:T(1,128)S(1)}, u32[]{:S(2)}, u32[]{:S(2)}) async-start(f32[16,1,4608]{2,1,0:T(1,128)} %reshape.239), calls=%async_computation.2 | async-start | bytes 589824 | tf_op jit(solution)/shard_map/all_to_all | solution.py:65
  13.1 4.4 %copy.56 = f32[2,2,128,16,32]{4,3,0,1,2:T(8,128)} copy(f32[2,2,128,16,32]{2,4,3,0,1:T(8,128)S(1)} %pad_maximum_fusion.1) | data formatting | bytes 2097152 | tf_op jit(solution)/shard_map/concatenate | solution.py:44
  17.5 4.7 %reshape.237 = f32[16,1,16384]{2,1,0:T(1,128)} reshape(f32[128,2,2,16,32]{4,3,2,1,0:T(8,128)} %bitcast.166) | data formatting | bytes 2097152
  22.2 5.7 %all-to-all-start = ((f32[16,1,16384]{2,1,0:T(1,128)}), f32[16,1,16384]{2,1,0:T(1,128)S(1)}, u32[]{:S(2)}, u32[]{:S(2)}) async-start(f32[16,1,16384]{2,1,0:T(1,128)} %reshape.237), calls=%async_computation | async-start | bytes 2097152 | tf_op jit(solution)/shard_map/all_to_all | solution.py:75
  32.4 11.0 %all-to-all-done = f32[16,1,16384]{2,1,0:T(1,128)S(1)} async-done(((f32[16,1,16384]{2,1,0:T(1,128)}), f32[16,1,16384]{2,1,0:T(1,128)S(1)}, u32[]{:S(2)}, u32[]{:S(2)}) %all-to-all-start) | async-done | bytes 1048608 | tf_op jit(solution)/shard_map/all_to_all | solution.py:75
  43.4 7.5 %all-to-all-start.3 = ((f32[8,2,16,512]{3,2,1,0:T(8,128)}), f32[8,2,16,512]{3,2,1,0:T(8,128)S(1)}, u32[]{:S(2)}, u32[]{:S(2)}) async-start(f32[8,2,16,512]{3,2,1,0:T(8,128)} %copy.64), calls=%async_computation.3 | async-start | bytes 1048576 | tf_op jit(solution)/shard_map/all_to_all | solution.py:68
  50.9 3.2 reduce
  54.1 2.7 reshape.238
  56.8 6.6 %copy.58 = f32[2,2,8,16,16,32]{5,4,3,1,2,0:T(8,128)} copy(f32[2,2,8,16,16,32]{5,3,0,1,2,4:T(8,128)} %bitcast.167) | data formatting | bytes 2097152 | tf_op jit(solution)/shard_map/all_to_all | solution.py:75
  63.4 3.5 %reshape.222 = f32[2,2,8,16,512,1]{4,3,1,2,0,5:T(8,128)S(1)} reshape(f32[2,2,8,16,16,32]{5,4,3,1,2,0:T(8,128)} %copy.58) | data formatting | bytes 2097152 | tf_op jit(solution)/shard_map/all_to_all | solution.py:75
  66.9 4.2 %convolution_bitcast_fusion.4 = f32[2,2,8,16,512]{4,3,1,2,0:T(8,128)S(1)} fusion(f32[2,512,2,512,1,1]{3,1,0,2,5,4:T(8,128)} %constant.84, f32[2,2,8,16,512,1]{4,3,1,2,0,5:T(8,128)S(1)} %reshape.222), kind=kOutput, calls=%fused_computation.7 | convolution fusion | flops 1610612736 | bytes 6291456 | tf_op jit(solution)/shard_map/fckxy,cydm->fdkxm/dot_general | solution.py:38
  73.0 6.6 %all-to-all-start.1 = ((f32[2,2,8,16,512]{4,3,1,0,2:T(8,128)}), f32[2,2,8,16,512]{4,3,1,0,2:T(8,128)S(1)}, u32[]{:S(2)}, u32[]{:S(2)}) async-start(f32[2,2,8,16,512]{4,3,1,0,2:T(8,128)} %copy.59), calls=%async_computation.1 | async-start | bytes 2097152 | tf_op jit(solution)/shard_map/all_to_all | solution.py:77
  80.9 16.1 %all-to-all-done.1 = f32[2,2,8,16,512]{4,3,1,0,2:T(8,128)S(1)} async-done(((f32[2,2,8,16,512]{4,3,1,0,2:T(8,128)}), f32[2,2,8,16,512]{4,3,1,0,2:T(8,128)S(1)}, u32[]{:S(2)}, u32[]{:S(2)}) %all-to-all-start.1) | async-done | bytes 1048608 | tf_op jit(solution)/shard_map/all_to_all | solution.py:77
  99.2 30.3 %all_to_all.105 = f32[2,2,1,128,512]{4,0,1,2,3:T(2,128)S(1)} all-to-all(f32[2,2,1,128,512]{4,0,1,2,3:T(2,128)S(1)} %copy.68), channel_id=1, replica_groups=mesh['px'=8,'py'=16] {'px'}, dimensions={3} | all-to-all | bytes 2097152 | tf_op jit(solution)/shard_map/all_to_all | solution.py:81
  129.5 2.4 convolution_bitcast_fusion.1
  131.9 8.8 %copy.71 = f32[2,2,8,16,512]{3,1,2,0,4:T(2,128)} copy(f32[2,2,8,16,512]{4,3,1,2,0:T(8,128)S(1)} %convolution_bitcast_fusion.1) | data formatting | bytes 2097152 | tf_op jit(solution)/shard_map/fckxm,cmdy->fdkxy/transpose | solution.py:38
  140.7 13.7 %reshape.241 = f32[16,1,16384]{2,1,0:T(1,128)} reshape(f32[512,2,8,2,16]{4,3,2,1,0:T(2,128)} %bitcast.162) | data formatting | bytes 2097152
  154.4 5.3 %all-to-all-start.5 = ((f32[16,1,16384]{2,1,0:T(1,128)}), f32[16,1,16384]{2,1,0:T(1,128)S(1)}, u32[]{:S(2)}, u32[]{:S(2)}) async-start(f32[16,1,16384]{2,1,0:T(1,128)} %reshape.241), calls=%async_computation.5 | async-start | bytes 2097152 | tf_op jit(solution)/shard_map/all_to_all | solution.py:83
  160.2 15.0 %all-to-all-done.5 = f32[16,1,16384]{2,1,0:T(1,128)S(1)} async-done(((f32[16,1,16384]{2,1,0:T(1,128)}), f32[16,1,16384]{2,1,0:T(1,128)S(1)}, u32[]{:S(2)}, u32[]{:S(2)}) %all-to-all-start.5) | async-done | bytes 1048608 | tf_op jit(solution)/shard_map/all_to_all | solution.py:83
  175.3 3.1 reduce.2
  178.4 13.2 %reshape.242 = f32[512,2,8,2,16]{4,3,2,1,0:T(2,128)} reshape(f32[16,16384]{1,0:T(8,128)S(1)} %reduce.2) | data formatting | bytes 2097152
  191.6 12.6 %copy.72 = f32[2,2,8,16,16,32]{5,3,2,4,1,0:T(8,128)} copy(f32[2,2,8,16,16,32]{3,1,2,0,5,4:T(2,128)} %bitcast.163) | data formatting | bytes 2097152 | tf_op jit(solution)/shard_map/all_to_all | solution.py:83
  204.2 4.4 %slice.102 = f32[2,2,127,16,32]{4,3,2,1,0:T(8,128)} slice(f32[2,2,128,16,32]{4,3,2,1,0:T(8,128)} %bitcast.164), slice={[0:2], [0:2], [1:128], [0:16], [0:32]} | slice | bytes 2080768 | tf_op jit(solution)/shard_map/slice | solution.py:44
  209.4 3.6 %copy.99 = f32[2,2,127,16,32]{2,4,1,3,0:T(8,128)S(1)} copy(f32[2,2,127,16,32]{4,3,2,1,0:T(8,128)} %slice.102) | data formatting | bytes 2080768
  214.2 68.4 %reshape.192 = f32[2,8,2,16,2,128,2]{6,5,4,3,2,1,0:T(8,128)} reshape(f32[2,16,32,256]{3,2,1,0:T(8,128)S(1)} %fusion.3) | data formatting | bytes 2097152 | tf_op jit(solution)/shard_map/reshape | solution.py:49
  282.6 20.8 %reduce_sum.27 = f32[2,8,16,128]{3,2,1,0:T(8,128)S(1)} reduce(f32[2,8,2,16,2,128,2]{6,5,4,3,2,1,0:T(8,128)} %reshape.192, f32[]{:T(128)} %constant.72.clone.1), dimensions={2,4,6}, to_apply=%region_0.1 | reduce | flops 229376 | bytes 1179652 | tf_op jit(solution)/shard_map/reduce_sum | solution.py:50
  303.4 9.9 %div.31 = f32[2,4,2,8,2,64,2]{6,5,4,3,2,1,0:T(8,128)} reshape(f32[2,8,16,128]{3,2,1,0:T(8,128)S(1)} %get-tuple-element.23) | data formatting | bytes 262144 | tf_op jit(solution)/shard_map/div | solution.py:50
  313.3 4.1 %reduce_sum.28 = f32[2,4,8,64]{3,2,1,0:T(8,128)S(1)} reduce(f32[2,4,2,8,2,64,2]{6,5,4,3,2,1,0:T(8,128)} %div.31, f32[]{:T(128)} %constant.72.clone.1), dimensions={2,4,6}, to_apply=%region_1.2 | reduce | flops 28672 | bytes 147460 | tf_op jit(solution)/shard_map/reduce_sum | solution.py:50
  319.6 4.4 %all-to-all-start.6 = ((f32[16,1,2336]{2,1,0:T(1,128)}), f32[16,1,2336]{2,1,0:T(1,128)S(1)}, u32[]{:S(2)}, u32[]{:S(2)}) async-start(f32[16,1,2336]{2,1,0:T(1,128)} %all_to_all.91), calls=%async_computation.6 | async-start | bytes 311296 | tf_op jit(solution)/shard_map/all_to_all | solution.py:96
  324.0 6.4 %all-to-all-done.6 = f32[16,1,2336]{2,1,0:T(1,128)S(1)} async-done(((f32[16,1,2336]{2,1,0:T(1,128)}), f32[16,1,2336]{2,1,0:T(1,128)S(1)}, u32[]{:S(2)}, u32[]{:S(2)}) %all-to-all-start.6) | async-done | bytes 149536 | tf_op jit(solution)/shard_map/all_to_all | solution.py:96
  332.6 9.3 %all_to_all.106 = f32[16,1,2336]{2,1,0:T(1,128)S(1)} all-to-all(f32[16,1,2336]{2,1,0:T(1,128)S(1)} %copy.75), channel_id=1, replica_groups=mesh['px'=8,'py'=16] {'py'}, dimensions={0} | all-to-all | bytes 299008 | tf_op jit(solution)/shard_map/all_to_all | solution.py:102
  (89 shorter events, 21.2 us)
Async XLA Ops:
  0.6 11.1 %copy-start = (f32[2,16,32,256]{3,2,1,0:T(8,128)S(1)}, f32[2,16,32,256]{3,2,1,0:T(8,128)}, u32[]{:S(2)}) copy-start(f32[2,16,32,256]{3,2,1,0:T(8,128)} %param.9) | copy-start | bytes 3145732
  0.6 11.1 %copy-start.5 = (f32[256,2,128,1,1]{2,0,4,3,1:T(8,128)S(1)}, f32[256,2,128,1,1]{2,0,4,3,1:T(8,128)}, u32[]{:S(2)}) copy-start(f32[256,2,128,1,1]{2,0,4,3,1:T(8,128)} %constant.83) | copy-start | bytes 786436
  4.5 17.7 %all-to-all-start.2 = ((f32[16,1,4608]{2,1,0:T(1,128)}), f32[16,1,4608]{2,1,0:T(1,128)S(1)}, u32[]{:S(2)}, u32[]{:S(2)}) async-start(f32[16,1,4608]{2,1,0:T(1,128)} %reshape.239), calls=%async_computation.2 | async-start | bytes 589824 | tf_op jit(solution)/shard_map/all_to_all | solution.py:65
  22.2 21.2 %all-to-all-start = ((f32[16,1,16384]{2,1,0:T(1,128)}), f32[16,1,16384]{2,1,0:T(1,128)S(1)}, u32[]{:S(2)}, u32[]{:S(2)}) async-start(f32[16,1,16384]{2,1,0:T(1,128)} %reshape.237), calls=%async_computation | async-start | bytes 2097152 | tf_op jit(solution)/shard_map/all_to_all | solution.py:75
  43.4 28.8 %all-to-all-start.3 = ((f32[8,2,16,512]{3,2,1,0:T(8,128)}), f32[8,2,16,512]{3,2,1,0:T(8,128)S(1)}, u32[]{:S(2)}, u32[]{:S(2)}) async-start(f32[8,2,16,512]{3,2,1,0:T(8,128)} %copy.64), calls=%async_computation.3 | async-start | bytes 1048576 | tf_op jit(solution)/shard_map/all_to_all | solution.py:68
  72.2 24.9 %copy-start.7 = (f32[2,128,2,128,1]{1,3,0,4,2:T(8,128)S(1)}, f32[2,128,2,128,1]{1,3,0,4,2:T(8,128)}, u32[]{:S(2)}) copy-start(f32[2,128,2,128,1]{1,3,0,4,2:T(8,128)} %constant.82) | copy-start | bytes 786436
  72.2 0.8 copy-start.3
  73.0 24.0 %all-to-all-start.1 = ((f32[2,2,8,16,512]{4,3,1,0,2:T(8,128)}), f32[2,2,8,16,512]{4,3,1,0,2:T(8,128)S(1)}, u32[]{:S(2)}, u32[]{:S(2)}) async-start(f32[2,2,8,16,512]{4,3,1,0,2:T(8,128)} %copy.59), calls=%async_computation.1 | async-start | bytes 2097152 | tf_op jit(solution)/shard_map/all_to_all | solution.py:77
  79.6 18.1 %copy-start.4 = (f32[2,128,2,128,1]{1,3,0,4,2:T(8,128)S(1)}, f32[2,128,2,128,1]{1,3,0,4,2:T(8,128)}, u32[]{:S(2)}) copy-start(f32[2,128,2,128,1]{1,3,0,4,2:T(8,128)} %constant.81) | copy-start | bytes 786436
  97.1 32.4 %copy-start.11 = (f32[2,512,2,512,1,1]{3,1,0,2,5,4:T(8,128)S(1)}, f32[2,512,2,512,1,1]{3,1,0,2,5,4:T(8,128)}, u32[]{:S(2)}) copy-start(f32[2,512,2,512,1,1]{3,1,0,2,5,4:T(8,128)} %constant.85) | copy-start | bytes 12582916
  140.7 19.0 %copy-start.8 = (s32[3,16]{1,0:T(4,128)S(1)}, s32[3,16]{1,0:T(4,128)}, u32[]{:S(2)}) copy-start(s32[3,16]{1,0:T(4,128)} %param.11) | copy-start | bytes 580
  154.4 20.9 %all-to-all-start.5 = ((f32[16,1,16384]{2,1,0:T(1,128)}), f32[16,1,16384]{2,1,0:T(1,128)S(1)}, u32[]{:S(2)}, u32[]{:S(2)}) async-start(f32[16,1,16384]{2,1,0:T(1,128)} %reshape.241), calls=%async_computation.5 | async-start | bytes 2097152 | tf_op jit(solution)/shard_map/all_to_all | solution.py:83
  208.6 4.9 %copy-start.6 = (f32[256,2,128,1,1]{2,0,1,4,3:T(8,128)S(1)}, f32[256,2,128,1,1]{2,0,1,4,3:T(8,128)}, u32[]{:S(2)}) copy-start(f32[256,2,128,1,1]{2,0,1,4,3:T(8,128)} %constant.86) | copy-start | bytes 786436
  214.2 68.4 %copy-start.2 = (f32[2,16,32,256]{3,2,1,0:T(8,128)}, f32[2,16,32,256]{3,2,1,0:T(8,128)S(1)}, u32[]{:S(2)}) copy-start(f32[2,16,32,256]{3,2,1,0:T(8,128)S(1)} %fusion.3) | copy-start | bytes 3145732
  313.3 10.7 %copy-start.10 = (s32[16]{0:T(128)S(1)}, s32[16]{0:T(128)}, u32[]{:S(2)}) copy-start(s32[16]{0:T(128)} %get-tuple-element.27) | copy-start | bytes 196
  313.3 10.7 %copy-start.9 = (s32[16]{0:T(128)S(1)}, s32[16]{0:T(128)}, u32[]{:S(2)}) copy-start(s32[16]{0:T(128)} %get-tuple-element.29) | copy-start | bytes 196
  313.3 30.6 %copy-start.1 = (f32[2,16,32,256]{3,2,1,0:T(8,128)S(1)}, f32[2,16,32,256]{3,2,1,0:T(8,128)}, u32[]{:S(2)}) copy-start(f32[2,16,32,256]{3,2,1,0:T(8,128)} %param.9) | copy-start | bytes 3145732
  319.6 10.8 %all-to-all-start.6 = ((f32[16,1,2336]{2,1,0:T(1,128)}), f32[16,1,2336]{2,1,0:T(1,128)S(1)}, u32[]{:S(2)}, u32[]{:S(2)}) async-start(f32[16,1,2336]{2,1,0:T(1,128)} %all_to_all.91), calls=%async_computation.6 | async-start | bytes 311296 | tf_op jit(solution)/shard_map/all_to_all | solution.py:96
where the time goes:
time: 346 us; the launch traced here: 344 us
  local copies, waits for them, and re-layouts  174 us (50%)
  waiting for transfers between devices  48.5 us (14%)
  blocking collectives  39.6 us (11%)
  starting transfers between devices  36.7 us (11%)
  other arithmetic  35.2 us (10%)
  matrix products  9.17 us (3%)
    reshape x1, local copies, waits for them, and re-layouts, coarsen(): values.reshape(members, size_x // 2, 2, size_y // 2, 2, size_z // 2, 2)  68.4 us
    unnamed x37, local copies, waits for them, and re-layouts  44 us
    all_to_all x1, blocking collectives, general_path(): lax.all_to_all(values, 'px', split_axis=3, concat_axis=2, tiled=True)  30.3 us
    reduce_sum x3, other arithmetic, coarsen(): return blocks.mean(axis=(2, 4, 6))  25 us
    all_to_all x1, waiting for transfers between devices, general_path(): lax.all_to_all(values, 'px', split_axis=2, concat_axis=3, tiled=True)  16.1 us
    all_to_all x1, waiting for transfers between devices, general_path(): lax.all_to_all(values, 'py', split_axis=4, concat_axis=2, tiled=True)  15 us
    all_to_all x1, local copies, waits for them, and re-layouts, general_path(): lax.all_to_all(values, 'py', split_axis=4, concat_axis=2, tiled=True)  12.6 us
    div x3, local copies, waits for them, and re-layouts, coarsen(): return blocks.mean(axis=(2, 4, 6))  11.1 us
  transfers between devices with their start and end apart: 6, of which 4 were waited for; matrix products, arithmetic and copies ran while one was open for 11% of the time, Pallas kernels for 0%

commit v1 on v0

v1 whole, which is shorter than its diff:
```python
import numpy as np

import jax
import jax.numpy as jnp
from jax import lax
from jax.experimental import pallas as pl
from jax.experimental.pallas import tpu as pltpu
from jax.sharding import PartitionSpec as P

MESH = pl.DeviceIdType.MESH
F32, BF16 = jnp.float32, jnp.bfloat16
PX, PY = 8, 16
DEV = PX * PY
LX, LY, LZ = 128, 512, 256
CX, CY = LX // PX, LY // PY
L = 128
QUAD = 4
HEIGHT = 24


def split(values):
    values = np.asarray(values, np.float32)
    high = values.astype(jnp.bfloat16)
    low = (values - high.astype(np.float32)).astype(jnp.bfloat16)
    return np.stack([high, low], 0)


def tables():
    k = np.arange(L)
    z = np.arange(LZ)
    angle = 2.0 * np.pi / LZ * (k[:, None] * z[None, :] % LZ)
    nyquist = np.where(z % 2 == 0, 1.0, -1.0)
    ahead = np.stack([np.cos(angle), -np.sin(angle)], 0)
    back = 2.0 * ahead
    ahead[1, 0] = nyquist
    back[0, 0] = 1.0
    back[1, 0] = nyquist
    z_ahead = split(ahead.reshape(LZ, LZ))
    z_back = split(back.reshape(LZ, LZ) / (LX * LY * LZ))
    first, second = k // 16, k % 16
    turn = first[:, None] * first[None, :] / 8.0 + second[:, None] * second[None, :] / 16.0
    cos, sin = np.cos(2 * np.pi * turn), -np.sin(2 * np.pi * turn)
    column = split(np.block([[cos, -sin], [sin, cos]]))
    row = split(np.block([[cos, sin], [-sin, cos]]))
    twiddle, small = [], []
    for t in range(QUAD):
        xl = (t // 2) * 8 + first
        yl = (t % 2) * 16 + second
        turn = first[:, None] * xl[None, :] / LX + second[:, None] * yl[None, :] / LY
        twiddle.append(np.stack([np.cos(2 * np.pi * turn), -np.sin(2 * np.pi * turn)], 0))
        turn = (t // 2) * first / 16.0 + (t % 2) * second / 32.0
        small.append(np.stack([np.cos(2 * np.pi * turn), -np.sin(2 * np.pi * turn)], 0))
    twiddle = np.concatenate(twiddle, 2).astype(np.float32)
    small = np.stack(small, 1).reshape(2 * QUAD, L).astype(np.float32)
    pool = np.zeros((LZ, LZ))
    pool[z, z // 2] = 1.0 / 8
    pool[z, 128 + z // 4] = 1.0 / 64
    pool[z, 192 + z // 8] = 1.0 / 512
    return [
        jnp.asarray(v)
        for v in (z_ahead, z_back, column, row, twiddle, small, pool.astype(jnp.bfloat16))
    ]


def parts(values):
    high = values.astype(BF16)
    return high, (values - high.astype(F32)).astype(BF16)


def product(left, right, dims):
    return lax.dot_general(left, right, (dims, ((), ())), preferred_element_type=F32)


def left_table(table, values, dims=((1,), (0,))):
    high, low = parts(values)
    first = product(table[0], high, dims) + product(table[0], low, dims)
    return first + product(table[1], high, dims)


def right_table(values, table, dims=((1,), (0,))):
    high, low = parts(values)
    first = product(high, table[0], dims) + product(low, table[0], dims)
    return first + product(high, table[1], dims)


def peer(index):
    return {"px": index // PY, "py": lax.rem(index, PY)}


def quarter(t):
    return slice((t // 2) * 8, (t // 2) * 8 + 8), slice((t % 2) * 16, (t % 2) * 16 + 16)


def tile(t):
    return slice(t * L, (t + 1) * L)


def butterfly(values):
    a, b, c, d = values
    p, q, r, s = a + b, a - b, c + d, c - d
    return [p + r, q + s, p - r, q - s]


def turned(real, imag, cos, sin):
    return real * cos - imag * sin, real * sin + imag * cos


def piece(index, height):
    return pl.ds(pl.multiple_of(index * height, height), height)


def kernel(
    group_ref, noise_ref, spec_ref, za_ref, zb_ref, col_ref, row_ref, tw_ref, small_ref, pool_ref,
    mod_ref, one_ref, two_ref, three_ref,
    s_send, s_recv, n_send, n_recv, u_table, v_table, ahead_send, ahead_recv, back_send, back_recv,
    half_y, c_send, c_recv, d_send, d_recv, local_sems, send_sems, recv_sems,
):
    me = lax.axis_index("px") * PY + lax.axis_index("py")
    my_py = lax.axis_index("py")
    barrier = pltpu.get_barrier_semaphore()

    @pl.loop(1, DEV)
    def _(away):
        other = lax.rem(me + away, DEV)
        pl.semaphore_signal(barrier, inc=1, device_id=peer(other), device_id_type=MESH)

    def spread(send, recv, height, slot):
        pltpu.make_async_copy(
            send.at[piece(me, height)], recv.at[piece(me, height)], local_sems.at[slot]
        ).start()

        @pl.loop(1, DEV)
        def _(away):
            other = lax.rem(me + away, DEV)
            pltpu.make_async_remote_copy(
                src_ref=send.at[piece(other, height)],
                dst_ref=recv.at[piece(me, height)],
                send_sem=send_sems.at[slot],
                recv_sem=recv_sems.at[slot],
                device_id=peer(other),
                device_id_type=MESH,
            ).start()

    def landed(send, recv, height, slot):
        pltpu.make_async_copy(
            send.at[piece(me, height)], recv.at[piece(me, height)], local_sems.at[slot]
        ).wait()
        rest = pl.ds(0, (DEV - 1) * height)
        whole = pltpu.make_async_remote_copy(
            src_ref=send.at[rest],
            dst_ref=recv.at[rest],
            send_sem=send_sems.at[slot],
            recv_sem=recv_sems.at[slot],
            device_id=peer(lax.rem(me + 1, DEV)),
            device_id_type=MESH,
        )
        whole.wait()

    for t in range(QUAD):
        xs, ys = quarter(t)
        block = spec_ref[xs, ys, :].reshape(L, LZ)
        s_send[pl.ds(t, L, stride=QUAD), :] = block[:, :L].T
        n_send[pl.ds(t, 1), :] = block[:, L:].T[:1]

    za = (za_ref[0], za_ref[1])

    def z_ahead(f):
        rows = [noise_ref[(f,) + quarter(t)].reshape(L, LZ) for t in range(QUAD)]
        return left_table(za, jnp.concatenate(rows, 0), ((1,), (1,)))

    values = [z_ahead(0), z_ahead(1)]
    at_zero = lax.broadcasted_iota(jnp.int32, (L, QUAD * L), 0) == 0
    real_one = jnp.where(at_zero, values[0][L:], values[1][:L])
    imag_zero = jnp.where(at_zero, values[1][:L], values[0][L:])
    members = ((values[0][:L], imag_zero), (real_one, values[1][L:]))
    for f in range(2):
        for c in range(2):
            for t in range(QUAD):
                ahead_send[f, pl.ds(c * QUAD + t, L, stride=8), :] = members[f][c][:, tile(t)]

    pl.semaphore_wait(barrier, DEV - 1)
    spread(s_send, s_recv, QUAD, 0)

    def last_copy(source):
        return pltpu.make_async_remote_copy(
            src_ref=n_send,
            dst_ref=n_recv.at[source],
            send_sem=send_sems.at[5],
            recv_sem=recv_sems.at[5],
            device_id={"px": 0, "py": 0},
            device_id_type=MESH,
        )

    pl.when(me != 0)(lambda: last_copy(me).start())
    spread(ahead_send.at[0], ahead_recv.at[0], 8, 1)
    spread(ahead_send.at[1], ahead_recv.at[1], 8, 2)

    landed(s_send, s_recv, QUAD, 0)
    for t in range(QUAD):
        u_table[t] = s_recv[pl.ds(t, L, stride=QUAD), :].T

    @pl.when(me != 0)
    def _():
        v_table[...] = u_table[...]
        last_copy(me).wait_send()

    @pl.when(me == 0)
    def _():
        n_recv[0] = n_send[...]
        whole = pltpu.make_async_remote_copy(
            src_ref=n_recv.at[pl.ds(1, DEV - 1)],
            dst_ref=n_recv.at[pl.ds(1, DEV - 1)],
            send_sem=send_sems.at[5],
            recv_sem=recv_sems.at[5],
            device_id={"px": 0, "py": 1},
            device_id_type=MESH,
        )
        whole.wait_recv()
        for t in range(QUAD):
            v_table[t] = n_recv[:, t, :].T

    column = (col_ref[0], col_ref[1])
    row = (row_ref[0], row_ref[1])
    for f in range(2):
        landed(ahead_send.at[f], ahead_recv.at[f], 8, 1 + f)
        plane = [
            jnp.concatenate(
                [ahead_recv[f, pl.ds(c * QUAD + t, L, stride=8), :] for t in range(QUAD)], 1
            )
            for c in range(2)
        ]
        mixed = left_table(column, jnp.concatenate(plane, 0))
        real, imag = turned(mixed[:L], mixed[L:], tw_ref[0], tw_ref[1])
        reals = butterfly([real[:, tile(t)] for t in range(QUAD)])
        imags = butterfly([imag[:, tile(t)] for t in range(QUAD)])
        rows = []
        for t in range(QUAD):
            cos, sin = small_ref[pl.ds(t, 1), :], small_ref[pl.ds(QUAD + t, 1), :]
            pair = turned(reals[t], imags[t], cos, sin) if t else (reals[t], imags[t])
            rows.append(jnp.concatenate(pair, 1))
        freq = right_table(jnp.concatenate(rows, 0), row)
        table = u_table if f == 0 else v_table
        scale = jnp.concatenate([table[t] for t in range(QUAD)], 0)
        freq = freq * jnp.concatenate([scale, scale], 1)
        mixed = right_table(freq, column)
        reals, imags = [], []
        for t in range(QUAD):
            part = mixed[tile(t)]
            pair = (part[:, :L], part[:, L:])
            if t:
                cos, sin = small_ref[pl.ds(t, 1), :], small_ref[pl.ds(QUAD + t, 1), :]
                pair = turned(*pair, cos, -sin)
            reals.append(pair[0])
            imags.append(pair[1])
        real = jnp.concatenate(butterfly(reals), 1)
        imag = jnp.concatenate(butterfly(imags), 1)
        real, imag = turned(real, imag, tw_ref[0], -tw_ref[1])
        plane = left_table(row, jnp.concatenate([real, imag], 0))
        for c in range(2):
            for t in range(QUAD):
                back_send[f, pl.ds(c * QUAD + t, L, stride=8), :] = plane[tile(c), tile(t)]
        spread(back_send.at[f], back_recv.at[f], 8, 3 + f)

    for f in range(2):
        landed(back_send.at[f], back_recv.at[f], 8, 3 + f)

    def slot(f, c):
        rows = [back_recv[f, pl.ds(c * QUAD + t, L, stride=8), :] for t in range(QUAD)]
        return jnp.concatenate(rows, 1)

    middle = (slot(0, 1), slot(1, 0))
    imag_zero = jnp.where(at_zero, middle[1], middle[0])
    real_one = jnp.where(at_zero, middle[0], middle[1])
    members = ((slot(0, 0), imag_zero), (real_one, slot(1, 1)))
    zb = (zb_ref[0], zb_ref[1])

    def fold(start, rows):
        for h in range(2):
            half_y[h, pl.ds(start, rows.shape[0]), :] = rows[:, tile(h)]

    for f in range(2):
        cells = right_table(jnp.concatenate(members[f], 0), zb, ((0,), (0,)))
        cells = jnp.exp(0.5 * cells)
        for t in range(QUAD):
            xs, ys = quarter(t)
            block = cells[tile(t)].reshape(8, 16, LZ)
            mod_ref[f, xs, ys, :] = block
            half_x = block.reshape(4, 2, 16, LZ)
            half_x = half_x[:, 0] + half_x[:, 1]
            for x in range(4):
                fold(((f * 2 + t // 2) * 4 + x) * CY + (t % 2) * 16, half_x[x])

    def pair_rows(count):
        rows = [
            half_y[h, pl.ds(0, count, stride=2), :] + half_y[h, pl.ds(1, count, stride=2), :]
            for h in range(2)
        ]
        return jnp.concatenate(rows, 1)

    def z_pool(values, lanes):
        high, low = parts(values)
        pool = pool_ref[:, lanes]
        return product(high, pool, ((1,), (0,))) + product(low, pool, ((1,), (0,)))

    rows_one = pair_rows(2 * 8 * 16)
    one = z_pool(rows_one, slice(0, 128))
    pairs = rows_one.reshape(2 * 4, 2, 16, LZ)
    fold(0, (pairs[:, 0] + pairs[:, 1]).reshape(2 * 4 * 16, LZ))
    rows_two = pair_rows(2 * 4 * 8)
    pairs = rows_two.reshape(2 * 2, 2, 8, LZ)
    fold(0, (pairs[:, 0] + pairs[:, 1]).reshape(2 * 2 * 8, LZ))
    rows_three = pair_rows(2 * 2 * 4)
    rest = z_pool(jnp.concatenate([rows_two, rows_three], 0), slice(128, 256))
    for i in range(PY):
        c_send[i, pl.ds(0, 16), :] = one[i * 16 : i * 16 + 16]
        c_send[i, pl.ds(16, 4), :] = rest[i * 4 : i * 4 + 4]
        c_send[i, pl.ds(20, 1), :] = rest[64 + i : 65 + i]
        c_send[i, pl.ds(21, 3), :] = jnp.zeros((3, L), F32)

    def across(send, recv, slot):
        copies = [pltpu.make_async_copy(send.at[my_py], recv.at[my_py], local_sems.at[slot])]
        for away in range(1, PY):
            other = lax.rem(my_py + away, PY)
            copies.append(
                pltpu.make_async_remote_copy(
                    src_ref=send.at[other],
                    dst_ref=recv.at[my_py],
                    send_sem=send_sems.at[slot + away],
                    recv_sem=recv_sems.at[slot + away],
                    device_id={"py": other},
                    device_id_type=MESH,
                )
            )
        for copy in copies:
            copy.start()
        for copy in copies:
            copy.wait()

    across(c_send, c_recv, 6)
    for g in range(PY):
        for level, rows in enumerate((pl.ds(0, 16), pl.ds(16, 4), pl.ds(20, 1))):
            d_send[g, rows, :] = c_recv[group_ref[level, g], rows, :]
        d_send[g, pl.ds(21, 3), :] = jnp.zeros((3, L), F32)
    across(d_send, d_recv, 6 + PY)
    for f in range(2):
        for x in range(8):
            one_ref[f, x] = d_recv[f * 8 + x, pl.ds(0, 16), :]
        for x in range(4):
            for h in range(2):
                i = (f * 4 + x) * 2 + h
                two_ref[f, x, pl.ds(h * 4, 4), :] = d_recv[i, pl.ds(16, 4), :][:, :64]
        for x in range(2):
            for y in range(4):
                three_ref[f, x, pl.ds(y, 1), :] = d_recv[(f * 2 + x) * 4 + y, pl.ds(20, 1), :][:, 64:96]


def on_device(white_noise, spectrum, group_table):
    shapes = [
        white_noise.shape,
        (2, CX // 2, CY // 2, LZ // 2),
        (2, CX // 4, CY // 4, LZ // 4),
        (2, CX // 8, CY // 8, LZ // 8),
    ]
    vmem = pl.BlockSpec(memory_space=pltpu.VMEM)
    wide = pltpu.VMEM((2, DEV * 8, L), F32)
    thin = pltpu.VMEM((DEV * QUAD, L), F32)
    coarse = pltpu.VMEM((PY, HEIGHT, L), F32)
    slots = 6 + 2 * PY
    return pl.pallas_call(
        kernel,
        out_shape=[jax.ShapeDtypeStruct(shape, F32) for shape in shapes],
        in_specs=[pl.BlockSpec(memory_space=pltpu.SMEM)] + [vmem] * 9,
        out_specs=[vmem] * 4,
        scratch_shapes=[
            thin, thin, pltpu.VMEM((QUAD, L), F32), pltpu.VMEM((DEV, QUAD, L), F32),
            pltpu.VMEM((QUAD, L, L), F32), pltpu.VMEM((QUAD, L, L), F32),
            wide, wide, wide, wide,
            pltpu.VMEM((2, 2 * 8 * CY, L), F32), coarse, coarse, coarse, coarse,
            pltpu.SemaphoreType.DMA((slots,)), pltpu.SemaphoreType.DMA((slots,)),
            pltpu.SemaphoreType.DMA((slots,)),
        ],
        compiler_params=pltpu.CompilerParams(
            collective_id=0, has_side_effects=True, vmem_limit_bytes=48 * 1024 * 1024
        ),
    )(group_table, white_noise, spectrum, *tables())


def solution(mesh):
    in_specs = (P(None, "px", "py", None), P("px", "py", None), P())
    out_specs = (P(None, "px", "py", None),) * 4
    return jax.shard_map(
        on_device, mesh=mesh, in_specs=in_specs, out_specs=out_specs, check_vma=False
    )
```

time: 346 us -> 81 us (0.23)
  local copies, waits for them, and re-layouts: 174 us -> 12.2 us
  Pallas kernels: 0 us -> 67.6 us
  waiting for transfers between devices: 48.5 us -> 0 us
  blocking collectives: 39.6 us -> 0 us
  starting transfers between devices: 36.7 us -> 0 us
  other arithmetic: 35.2 us -> 0 us
  matrix products: 9.17 us -> 0 us
    reshape x4 -> x0, local copies, waits for them, and re-layouts: 69.5 us -> none  [the longest x1 68.4 us: coarsen(): values.reshape(members, size_x // 2, 2, size_y // 2, 2, size_z // 2, 2)]
    pallas_call x0 -> x1, Pallas kernels: none -> 67.6 us  [on_device(): pl.pallas_call(kernel, out_shape=[jax.ShapeDtypeStruct(shape, F32) for sh...]
    all_to_all x6 -> x0, waiting for transfers between devices: 48.5 us -> none  [the longest x1 16.1 us: general_path(): lax.all_to_all(values, 'px', split_axis=2, concat_axis=3, tiled=True)]
    all_to_all x2 -> x0, blocking collectives: 39.6 us -> none  [the longest x1 30.3 us: general_path(): lax.all_to_all(values, 'px', split_axis=3, concat_axis=2, tiled=True)]
    all_to_all x6 -> x0, starting transfers between devices: 36.7 us -> none  [the longest x1 7.5 us: general_path(): lax.all_to_all(table, 'px', split_axis=0, concat_axis=2, tiled=True)[0]]
    unnamed x37 -> x24, local copies, waits for them, and re-layouts: 44 us -> 12.2 us
    reduce_sum x3 -> x0, other arithmetic: 25 us -> none  [coarsen(): return blocks.mean(axis=(2, 4, 6))]
    all_to_all x7 -> x0, local copies, waits for them, and re-layouts: 24.2 us -> none  [the longest x1 12.6 us: general_path(): lax.all_to_all(values, 'py', split_axis=4, concat_axis=2, tiled=True)]
  transfers between devices with their start and end apart: 6 -> 0, of which waited for: 4 -> 0; matrix products, arithmetic and copies ran while one was open for 11% -> 0% of each run, Pallas kernels for 0% -> 0%
where the time goes in v1:
time: 81 us; the launch traced here: 80.5 us
  Pallas kernels  67.6 us (83%)
  local copies, waits for them, and re-layouts  12.2 us (15%)
    pallas_call x1, Pallas kernels, on_device(): pl.pallas_call(kernel, out_shape=[jax.ShapeDtypeStruct(shape, F32) for sh...  67.6 us
    unnamed x24, local copies, waits for them, and re-layouts  12.2 us

profile of v1, /device:TPU:1, one launch (start us, length us, event | category | flops | bytes accessed | tf_op | source)
XLA Modules:
  0.0 80.5 jit_solution(13545009630738725069)
XLA Ops:
  0.6 0.0 copy-start.8
  0.6 0.7 copy-done.8
  1.3 0.0 copy-start
  1.3 1.2 %copy-done = f32[2,16,32,256]{3,2,1,0:T(8,128)S(1)} copy-done((f32[2,16,32,256]{3,2,1,0:T(8,128)S(1)}, f32[2,16,32,256]{3,2,1,0:T(8,128)}, u32[]{:S(2)}) %copy-start) | copy-done | bytes 1048600
  2.5 0.0 copy-start.1
  2.5 1.0 %copy-done.1 = f32[16,32,256]{2,1,0:T(8,128)S(1)} copy-done((f32[16,32,256]{2,1,0:T(8,128)S(1)}, f32[16,32,256]{2,1,0:T(8,128)}, u32[]{:S(2)}) %copy-start.1) | copy-done | bytes 524312
  3.6 0.0 copy-start.2
  3.6 1.0 %copy-done.2 = f32[2,128,512]{2,1,0:T(8,128)S(1)} copy-done((f32[2,128,512]{2,1,0:T(8,128)S(1)}, f32[2,128,512]{2,1,0:T(8,128)}, u32[]{:S(2)}) %copy-start.2) | copy-done | bytes 524312
  4.6 0.0 copy-start.3
  4.6 0.9 %copy-done.3 = bf16[2,256,256]{2,1,0:T(8,128)(2,1)S(1)} copy-done((bf16[2,256,256]{2,1,0:T(8,128)(2,1)S(1)}, bf16[2,256,256]{2,1,0:T(8,128)(2,1)}, u32[]{:S(2)}) %copy-start.3) | copy-done | bytes 262168
  5.6 0.0 copy-start.4
  5.6 0.9 %copy-done.4 = bf16[2,256,256]{2,1,0:T(8,128)(2,1)S(1)} copy-done((bf16[2,256,256]{2,1,0:T(8,128)(2,1)S(1)}, bf16[2,256,256]{2,1,0:T(8,128)(2,1)}, u32[]{:S(2)}) %copy-start.4) | copy-done | bytes 262168
  6.5 0.0 copy-start.5
  6.5 0.9 %copy-done.5 = bf16[2,256,256]{2,1,0:T(8,128)(2,1)S(1)} copy-done((bf16[2,256,256]{2,1,0:T(8,128)(2,1)S(1)}, bf16[2,256,256]{2,1,0:T(8,128)(2,1)}, u32[]{:S(2)}) %copy-start.5) | copy-done | bytes 262168
  7.5 0.0 copy-start.6
  7.5 0.9 %copy-done.6 = bf16[2,256,256]{2,1,0:T(8,128)(2,1)S(1)} copy-done((bf16[2,256,256]{2,1,0:T(8,128)(2,1)S(1)}, bf16[2,256,256]{2,1,0:T(8,128)(2,1)}, u32[]{:S(2)}) %copy-start.6) | copy-done | bytes 262168
  8.4 0.0 copy-start.7
  8.4 0.9 %copy-done.7 = bf16[256,256]{1,0:T(8,128)(2,1)S(1)} copy-done((bf16[256,256]{1,0:T(8,128)(2,1)S(1)}, bf16[256,256]{1,0:T(8,128)(2,1)}, u32[]{:S(2)}) %copy-start.7) | copy-done | bytes 131096
  9.3 0.0 copy-start.9
  9.3 0.7 copy-done.9
  10.0 67.6 %shard_map.129 = (f32[2,16,32,256]{3,2,1,0:T(8,128)S(1)}, f32[2,8,16,128]{3,2,1,0:T(8,128)S(1)}, f32[2,4,8,64]{3,2,1,0:T(8,128)S(1)}, f32[2,2,4,32]{3,2,1,0:T(4,128)S(1)}) custom-call(s32[3,16]{1,0:T(4,128)S(1)} %copy-done.9, f32[2,16,32,256]{3,2,1,0:T(8,128)S(1)} %copy-done, f32[16,32,256]{2,1,0:T(8,128)S(1)} %copy-done.1, ...), custom_call_target="tpu_custom_call" | custom-call | tf_op jit(solution)/shard_map/pallas_call | solution.py:369
  77.7 1.0 %copy.18 = f32[2,16,32,256]{3,2,1,0:T(8,128)} copy(f32[2,16,32,256]{3,2,1,0:T(8,128)S(1)} %get-tuple-element.8) | data formatting | bytes 2097152
  78.6 0.7 copy.19
  79.3 0.6 copy.20
  79.9 0.6 copy.21
Async XLA Ops:
  0.6 0.7 copy-start.8
  1.3 1.2 %copy-start = (f32[2,16,32,256]{3,2,1,0:T(8,128)S(1)}, f32[2,16,32,256]{3,2,1,0:T(8,128)}, u32[]{:S(2)}) copy-start(f32[2,16,32,256]{3,2,1,0:T(8,128)} %noise_ref.1) | copy-start | bytes 3145732
  2.5 1.0 %copy-start.1 = (f32[16,32,256]{2,1,0:T(8,128)S(1)}, f32[16,32,256]{2,1,0:T(8,128)}, u32[]{:S(2)}) copy-start(f32[16,32,256]{2,1,0:T(8,128)} %spec_ref.1) | copy-start | bytes 1572868
  3.6 1.0 %copy-start.2 = (f32[2,128,512]{2,1,0:T(8,128)S(1)}, f32[2,128,512]{2,1,0:T(8,128)}, u32[]{:S(2)}) copy-start(f32[2,128,512]{2,1,0:T(8,128)} %constant.18.clone.tw_ref) | copy-start | bytes 1572868
  4.6 0.9 %copy-start.3 = (bf16[2,256,256]{2,1,0:T(8,128)(2,1)S(1)}, bf16[2,256,256]{2,1,0:T(8,128)(2,1)}, u32[]{:S(2)}) copy-start(bf16[2,256,256]{2,1,0:T(8,128)(2,1)} %constant.17.clone.row_ref) | copy-start | bytes 786436
  5.6 0.9 %copy-start.4 = (bf16[2,256,256]{2,1,0:T(8,128)(2,1)S(1)}, bf16[2,256,256]{2,1,0:T(8,128)(2,1)}, u32[]{:S(2)}) copy-start(bf16[2,256,256]{2,1,0:T(8,128)(2,1)} %constant.16.clone.col_ref) | copy-start | bytes 786436
  6.5 0.9 %copy-start.5 = (bf16[2,256,256]{2,1,0:T(8,128)(2,1)S(1)}, bf16[2,256,256]{2,1,0:T(8,128)(2,1)}, u32[]{:S(2)}) copy-start(bf16[2,256,256]{2,1,0:T(8,128)(2,1)} %constant.15.clone.zb_ref) | copy-start | bytes 786436
  7.5 0.9 %copy-start.6 = (bf16[2,256,256]{2,1,0:T(8,128)(2,1)S(1)}, bf16[2,256,256]{2,1,0:T(8,128)(2,1)}, u32[]{:S(2)}) copy-start(bf16[2,256,256]{2,1,0:T(8,128)(2,1)} %constant.14.clone.za_ref) | copy-start | bytes 786436
  8.4 0.9 %copy-start.7 = (bf16[256,256]{1,0:T(8,128)(2,1)S(1)}, bf16[256,256]{1,0:T(8,128)(2,1)}, u32[]{:S(2)}) copy-start(bf16[256,256]{1,0:T(8,128)(2,1)} %constant.20.clone.pool_ref) | copy-start | bytes 393220
  9.3 0.7 copy-start.9

commit v2 on v1

--- a/solution.py
+++ b/solution.py
@@ -83,8 +83,16 @@
     return first + product(high, table[1], dims)
 
 
-def peer(index):
-    return {"px": index // PY, "py": lax.rem(index, PY)}
+def place():
+    px, py = lax.axis_index("px"), lax.axis_index("py")
+    return (px >> 2) * 2 + ((py >> 1) & 1), px & 3, py >> 2, py & 1
+
+
+def shifted(here, dz, dy, dx, dc):
+    z, y, x = ((here[i] + d) & 3 for i, d in enumerate((dz, dy, dx)))
+    px = (z >> 1) * 4 + y
+    py = x * 4 + (z & 1) * 2 + (here[3] ^ dc)
+    return px * PY + py, {"px": px, "py": py}
 
 
 def quarter(t):
@@ -110,36 +118,58 @@
 
 
 def kernel(
+    group_in, noise_in, spec_in, za_in, zb_in, col_in, row_in, tw_in, small_in, pool_in,
+    mod_ref, one_ref, two_ref, three_ref,
     group_ref, noise_ref, spec_ref, za_ref, zb_ref, col_ref, row_ref, tw_ref, small_ref, pool_ref,
-    mod_ref, one_ref, two_ref, three_ref,
     s_send, s_recv, n_send, n_recv, u_table, v_table, ahead_send, ahead_recv, back_send, back_recv,
-    half_y, c_send, c_recv, d_send, d_recv, local_sems, send_sems, recv_sems,
+    half_y, c_send, c_recv, d_send, d_recv, all_sem, fetch_sems, local_sems, send_sems, recv_sems,
 ):
-    me = lax.axis_index("px") * PY + lax.axis_index("py")
-    my_py = lax.axis_index("py")
+    here = place()
+    my_px, my_py = lax.axis_index("px"), lax.axis_index("py")
+    me = my_px * PY + my_py
     barrier = pltpu.get_barrier_semaphore()
 
-    @pl.loop(1, DEV)
-    def _(away):
-        other = lax.rem(me + away, DEV)
-        pl.semaphore_signal(barrier, inc=1, device_id=peer(other), device_id_type=MESH)
+    for away in range(1, PY):
+        other = {"py": (my_py + away) & (PY - 1)}
+        pl.semaphore_signal(barrier, inc=1, device_id=other, device_id_type=MESH)
+    lines = [{"px": (my_px + away) & (PX - 1)} for away in range(1, PX)]
+    for other in lines:
+        pl.semaphore_signal(barrier, inc=1, device_id=other, device_id_type=MESH)
+    pairs = (
+        (spec_in, spec_ref), (noise_in, noise_ref), (za_in, za_ref), (col_in, col_ref),
+        (row_in, row_ref), (tw_in, tw_ref), (small_in, small_ref), (zb_in, zb_ref),
+        (pool_in, pool_ref), (group_in, group_ref),
+    )
+    fetches = [
+        pltpu.make_async_copy(source, target, fetch_sems.at[index])
+        for index, (source, target) in enumerate(pairs)
+    ]
+    for fetch in fetches:
+        fetch.start()
 
     def spread(send, recv, height, slot):
         pltpu.make_async_copy(
             send.at[piece(me, height)], recv.at[piece(me, height)], local_sems.at[slot]
         ).start()
 
-        @pl.loop(1, DEV)
-        def _(away):
-            other = lax.rem(me + away, DEV)
+        def send_to(shift):
+            other, device = shifted(here, *shift)
             pltpu.make_async_remote_copy(
                 src_ref=send.at[piece(other, height)],
                 dst_ref=recv.at[piece(me, height)],
                 send_sem=send_sems.at[slot],
                 recv_sem=recv_sems.at[slot],
-                device_id=peer(other),
+                device_id=device,
                 device_id_type=MESH,
             ).start()
+
+        @pl.loop(0, 16)
+        def _(step):
+            dx, dy = step & 3, step >> 2
+            pl.when(step != 0)(lambda: send_to((0, dy, dx, 0)))
+            for n in range(1, 8):
+                dz, dc = n >> 1, n & 1
+                send_to((dz, dy + n, dx + dz, dc))
 
     def landed(send, recv, height, slot):
         pltpu.make_async_copy(
@@ -151,17 +181,24 @@
             dst_ref=recv.at[rest],
             send_sem=send_sems.at[slot],
             recv_sem=recv_sems.at[slot],
-            device_id=peer(lax.rem(me + 1, DEV)),
+            device_id=shifted(here, 0, 0, 0, 1)[1],
             device_id_type=MESH,
         )
         whole.wait()
 
+    fetches[0].wait()
     for t in range(QUAD):
         xs, ys = quarter(t)
         block = spec_ref[xs, ys, :].reshape(L, LZ)
         s_send[pl.ds(t, L, stride=QUAD), :] = block[:, :L].T
         n_send[pl.ds(t, 1), :] = block[:, L:].T[:1]
 
+    pl.semaphore_wait(barrier, PX + PY - 2)
+    for other in lines:
+        pl.semaphore_signal(all_sem, inc=1, device_id=other, device_id_type=MESH)
+
+    fetches[1].wait()
+    fetches[2].wait()
     za = (za_ref[0], za_ref[1])
 
     def z_ahead(f):
@@ -178,7 +215,7 @@
             for t in range(QUAD):
                 ahead_send[f, pl.ds(c * QUAD + t, L, stride=8), :] = members[f][c][:, tile(t)]
 
-    pl.semaphore_wait(barrier, DEV - 1)
+    pl.semaphore_wait(all_sem, PX - 1)
     spread(s_send, s_recv, QUAD, 0)
 
     def last_copy(source):
@@ -219,6 +256,8 @@
         for t in range(QUAD):
             v_table[t] = n_recv[:, t, :].T
 
+    for index in range(3, 7):
+        fetches[index].wait()
     column = (col_ref[0], col_ref[1])
     row = (row_ref[0], row_ref[1])
     for f in range(2):
@@ -268,6 +307,8 @@
         rows = [back_recv[f, pl.ds(c * QUAD + t, L, stride=8), :] for t in range(QUAD)]
         return jnp.concatenate(rows, 1)
 
+    for index in range(7, 10):
+        fetches[index].wait()
     middle = (slot(0, 1), slot(1, 0))
     imag_zero = jnp.where(at_zero, middle[1], middle[0])
     real_one = jnp.where(at_zero, middle[0], middle[1])
@@ -362,27 +403,31 @@
         (2, CX // 8, CY // 8, LZ // 8),
     ]
     vmem = pl.BlockSpec(memory_space=pltpu.VMEM)
+    hbm = pl.BlockSpec(memory_space=pltpu.HBM)
     wide = pltpu.VMEM((2, DEV * 8, L), F32)
     thin = pltpu.VMEM((DEV * QUAD, L), F32)
     coarse = pltpu.VMEM((PY, HEIGHT, L), F32)
     slots = 6 + 2 * PY
+    operands = [white_noise, spectrum] + tables()
     return pl.pallas_call(
         kernel,
         out_shape=[jax.ShapeDtypeStruct(shape, F32) for shape in shapes],
-        in_specs=[pl.BlockSpec(memory_space=pltpu.SMEM)] + [vmem] * 9,
+        in_specs=[hbm] * (len(operands) + 1),
         out_specs=[vmem] * 4,
-        scratch_shapes=[
+        scratch_shapes=[pltpu.SMEM(group_table.shape, jnp.int32)]
+        + [pltpu.VMEM(value.shape, value.dtype) for value in operands]
+        + [
             thin, thin, pltpu.VMEM((QUAD, L), F32), pltpu.VMEM((DEV, QUAD, L), F32),
             pltpu.VMEM((QUAD, L, L), F32), pltpu.VMEM((QUAD, L, L), F32),
             wide, wide, wide, wide,
             pltpu.VMEM((2, 2 * 8 * CY, L), F32), coarse, coarse, coarse, coarse,
-            pltpu.SemaphoreType.DMA((slots,)), pltpu.SemaphoreType.DMA((slots,)),
+            pltpu.SemaphoreType.REGULAR, pltpu.SemaphoreType.DMA((len(operands) + 1,)), pltpu.SemaphoreType.DMA((slots,)), pltpu.SemaphoreType.DMA((slots,)),
             pltpu.SemaphoreType.DMA((slots,)),
         ],
         compiler_params=pltpu.CompilerParams(
-            collective_id=0, has_side_effects=True, vmem_limit_bytes=48 * 1024 * 1024
+            collective_id=0, has_side_effects=True, vmem_limit_bytes=67_043_328
         ),
-    )(group_table, white_noise, spectrum, *tables())
+    )(group_table, *operands)
 
 
 def solution(mesh):

time: 81 us -> 61.6 us (0.76)
  Pallas kernels: 67.6 us -> 56.3 us
  local copies, waits for them, and re-layouts: 12.2 us -> 4.41 us
    pallas_call x1, Pallas kernels: 67.6 us -> 56.3 us  [on_device(): pl.pallas_call(kernel, out_shape=[jax.ShapeDtypeStruct(shape, F32) for sh...]
    unnamed x24 -> x10, local copies, waits for them, and re-layouts: 12.2 us -> 4.41 us
where the time goes in v2:
time: 61.6 us; the launch traced here: 61.4 us
  Pallas kernels  56.3 us (91%)
  local copies, waits for them, and re-layouts  4.41 us (7%)
  between operations  0.65 us (1%)
    pallas_call x1, Pallas kernels, on_device(): pl.pallas_call(kernel, out_shape=[jax.ShapeDtypeStruct(shape, F32) for sh...  56.3 us
    unnamed x10, local copies, waits for them, and re-layouts  4.41 us

profile of v2, /device:TPU:1, one launch (start us, length us, event | category | flops | bytes accessed | tf_op | source)
XLA Modules:
  0.0 61.4 jit_solution(2089122682202659833)
XLA Ops:
  0.6 56.3 %shard_map.129 = (f32[2,16,32,256]{3,2,1,0:T(8,128)}, f32[2,8,16,128]{3,2,1,0:T(8,128)}, f32[2,4,8,64]{3,2,1,0:T(8,128)}, f32[2,2,4,32]{3,2,1,0:T(4,128)}) custom-call(s32[3,16]{1,0:T(4,128)} %group_in.1, f32[2,16,32,256]{3,2,1,0:T(8,128)} %noise_in.1, f32[16,32,256]{2,1,0:T(8,128)} %spec_in.1, bf16[2,256,256]{2,1,0:T(8,128)(2,1)} %constant.14.clone.za_in, ...), custom_call_target="tpu_custom_call" | custom-call | tf_op jit(solution)/shard_map/pallas_call | solution.py:412
  56.9 0.0 copy-start
  57.0 2.3 %copy.18 = f32[2,16,32,256]{3,2,1,0:T(8,128)} copy(f32[2,16,32,256]{3,2,1,0:T(8,128)} %get-tuple-element.8) | data formatting | bytes 2097152
  59.3 0.0 copy-done
  59.3 0.0 copy-start.1
  59.3 0.7 %copy.19 = f32[2,8,16,128]{3,2,1,0:T(8,128)} copy(f32[2,8,16,128]{3,2,1,0:T(8,128)S(1)} %copy-done) | data formatting | bytes 262144
  60.0 0.1 copy-done.1
  60.1 0.0 copy-start.2
  60.1 0.6 %copy.20 = f32[2,4,8,64]{3,2,1,0:T(8,128)} copy(f32[2,4,8,64]{3,2,1,0:T(8,128)S(1)} %copy-done.1) | data formatting | bytes 32768
  60.7 0.1 copy-done.2
  60.8 0.6 copy.21
Async XLA Ops:
  56.9 2.4 %copy-start = (f32[2,8,16,128]{3,2,1,0:T(8,128)S(1)}, f32[2,8,16,128]{3,2,1,0:T(8,128)}, u32[]{:S(2)}) copy-start(f32[2,8,16,128]{3,2,1,0:T(8,128)} %get-tuple-element.9) | copy-start | bytes 393220
  59.3 0.8 %copy-start.1 = (f32[2,4,8,64]{3,2,1,0:T(8,128)S(1)}, f32[2,4,8,64]{3,2,1,0:T(8,128)}, u32[]{:S(2)}) copy-start(f32[2,4,8,64]{3,2,1,0:T(8,128)} %get-tuple-element.10) | copy-start | bytes 49156
  60.1 0.7 %copy-start.2 = (f32[2,2,4,32]{3,2,1,0:T(4,128)S(1)}, f32[2,2,4,32]{3,2,1,0:T(4,128)}, u32[]{:S(2)}) copy-start(f32[2,2,4,32]{3,2,1,0:T(4,128)} %get-tuple-element.11) | copy-start | bytes 6148

commit v3 on v2

--- a/solution.py
+++ b/solution.py
@@ -15,7 +15,6 @@
 CX, CY = LX // PX, LY // PY
 L = 128
 QUAD = 4
-HEIGHT = 24
 
 
 def split(values):
@@ -83,6 +82,18 @@
     return first + product(high, table[1], dims)
 
 
+def hops(shift):
+    return sum(min(d, 4 - d) for d in shift[:3])
+
+
+SHIFTS = [(dz, dy, dx, dc) for dz in range(4) for dy in range(4) for dx in range(4) for dc in range(2)]
+MIXED = [SHIFTS[(i * 37) % 128] for i in range(1, 128)]
+SHIFTS = sorted(SHIFTS[1:], key=lambda shift: -hops(shift))
+
+LINE = [(dx, low) for dx in range(4) for low in range(4)]
+LINE = sorted(LINE[1:], key=lambda move: -min(move[0], 4 - move[0]) - (move[1] >> 1))
+
+
 def place():
     px, py = lax.axis_index("px"), lax.axis_index("py")
     return (px >> 2) * 2 + ((py >> 1) & 1), px & 3, py >> 2, py & 1
@@ -119,22 +130,17 @@
 
 def kernel(
     group_in, noise_in, spec_in, za_in, zb_in, col_in, row_in, tw_in, small_in, pool_in,
-    mod_ref, one_ref, two_ref, three_ref,
+    mod_out, one_out, rest_out,
     group_ref, noise_ref, spec_ref, za_ref, zb_ref, col_ref, row_ref, tw_ref, small_ref, pool_ref,
-    s_send, s_recv, n_send, n_recv, u_table, v_table, ahead_send, ahead_recv, back_send, back_recv,
-    half_y, c_send, c_recv, d_send, d_recv, all_sem, fetch_sems, local_sems, send_sems, recv_sems,
+    s_send, s_recv, n_send, n_line, n_recv, u_table, v_table, ahead_send, ahead_recv, back_send, back_recv,
+    mod_ref, half_y, one_send, one_recv_0, one_recv_1, one_back, rest_send, rest_recv, rest_back,
+    fetch_sems, local_sems, send_sems, recv_sems,
 ):
     here = place()
     my_px, my_py = lax.axis_index("px"), lax.axis_index("py")
     me = my_px * PY + my_py
     barrier = pltpu.get_barrier_semaphore()
 
-    for away in range(1, PY):
-        other = {"py": (my_py + away) & (PY - 1)}
-        pl.semaphore_signal(barrier, inc=1, device_id=other, device_id_type=MESH)
-    lines = [{"px": (my_px + away) & (PX - 1)} for away in range(1, PX)]
-    for other in lines:
-        pl.semaphore_signal(barrier, inc=1, device_id=other, device_id_type=MESH)
     pairs = (
         (spec_in, spec_ref), (noise_in, noise_ref), (za_in, za_ref), (col_in, col_ref),
         (row_in, row_ref), (tw_in, tw_ref), (small_in, small_ref), (zb_in, zb_ref),
@@ -147,7 +153,10 @@
     for fetch in fetches:
         fetch.start()
 
-    def spread(send, recv, height, slot):
+    for shift in SHIFTS:
+        pl.semaphore_signal(barrier, inc=1, device_id=shifted(here, *shift)[1], device_id_type=MESH)
+
+    def spread(send, recv, height, slot, order=MIXED):
         pltpu.make_async_copy(
             send.at[piece(me, height)], recv.at[piece(me, height)], local_sems.at[slot]
         ).start()
@@ -163,13 +172,8 @@
                 device_id_type=MESH,
             ).start()
 
-        @pl.loop(0, 16)
-        def _(step):
-            dx, dy = step & 3, step >> 2
-            pl.when(step != 0)(lambda: send_to((0, dy, dx, 0)))
-            for n in range(1, 8):
-                dz, dc = n >> 1, n & 1
-                send_to((dz, dy + n, dx + dz, dc))
+        for shift in order:
+            send_to(shift)
 
     def landed(send, recv, height, slot):
         pltpu.make_async_copy(
@@ -193,10 +197,6 @@
         s_send[pl.ds(t, L, stride=QUAD), :] = block[:, :L].T
         n_send[pl.ds(t, 1), :] = block[:, L:].T[:1]
 
-    pl.semaphore_wait(barrier, PX + PY - 2)
-    for other in lines:
-        pl.semaphore_signal(all_sem, inc=1, device_id=other, device_id_type=MESH)
-
     fetches[1].wait()
     fetches[2].wait()
     za = (za_ref[0], za_ref[1])
@@ -215,53 +215,87 @@
             for t in range(QUAD):
                 ahead_send[f, pl.ds(c * QUAD + t, L, stride=8), :] = members[f][c][:, tile(t)]
 
-    pl.semaphore_wait(all_sem, PX - 1)
-    spread(s_send, s_recv, QUAD, 0)
-
-    def last_copy(source):
-        return pltpu.make_async_remote_copy(
-            src_ref=n_send,
-            dst_ref=n_recv.at[source],
-            send_sem=send_sems.at[5],
-            recv_sem=recv_sems.at[5],
-            device_id={"px": 0, "py": 0},
+    pl.semaphore_wait(barrier, DEV - 1)
+    line_copy = pltpu.make_async_remote_copy(
+        src_ref=n_send,
+        dst_ref=n_line.at[my_py],
+        send_sem=send_sems.at[5],
+        recv_sem=recv_sems.at[5],
+        device_id={"py": 0},
+        device_id_type=MESH,
+    )
+    plane_copies = [
+        pltpu.make_async_remote_copy(
+            src_ref=n_line.at[i],
+            dst_ref=n_recv.at[my_px * PY + i],
+            send_sem=send_sems.at[6],
+            recv_sem=recv_sems.at[6],
+            device_id={"px": 0},
             device_id_type=MESH,
         )
-
-    pl.when(me != 0)(lambda: last_copy(me).start())
+        for i in range(PY)
+    ]
+
+    def line_rest(device):
+        rest = n_line.at[pl.ds(1, PY - 1)]
+        return pltpu.make_async_remote_copy(
+            src_ref=rest, dst_ref=rest, send_sem=send_sems.at[5], recv_sem=recv_sems.at[5],
+            device_id=device, device_id_type=MESH,
+        )
+
+    def plane_rest(rest, device):
+        return pltpu.make_async_remote_copy(
+            src_ref=rest, dst_ref=rest, send_sem=send_sems.at[6], recv_sem=recv_sems.at[6],
+            device_id=device, device_id_type=MESH,
+        )
+
+    pl.when(my_py != 0)(line_copy.start)
+    spread(s_send, s_recv, QUAD, 0)
+
     spread(ahead_send.at[0], ahead_recv.at[0], 8, 1)
+
+    @pl.when(my_py == 0)
+    def _():
+        n_line[0] = n_send[...]
+        line_rest({"py": 1}).wait_recv()
+
+        @pl.when(my_px != 0)
+        def _():
+            for copy in plane_copies:
+                copy.start()
+
     spread(ahead_send.at[1], ahead_recv.at[1], 8, 2)
 
     landed(s_send, s_recv, QUAD, 0)
     for t in range(QUAD):
         u_table[t] = s_recv[pl.ds(t, L, stride=QUAD), :].T
 
-    @pl.when(me != 0)
-    def _():
-        v_table[...] = u_table[...]
-        last_copy(me).wait_send()
-
-    @pl.when(me == 0)
-    def _():
-        n_recv[0] = n_send[...]
-        whole = pltpu.make_async_remote_copy(
-            src_ref=n_recv.at[pl.ds(1, DEV - 1)],
-            dst_ref=n_recv.at[pl.ds(1, DEV - 1)],
-            send_sem=send_sems.at[5],
-            recv_sem=recv_sems.at[5],
-            device_id={"px": 0, "py": 1},
-            device_id_type=MESH,
-        )
-        whole.wait_recv()
-        for t in range(QUAD):
-            v_table[t] = n_recv[:, t, :].T
-
+    pl.when(my_py != 0)(line_copy.wait_send)
     for index in range(3, 7):
         fetches[index].wait()
+
+    def last_table():
+        @pl.when(me != 0)
+        def _():
+            v_table[...] = u_table[...]
+
+        @pl.when((my_py == 0) & (my_px != 0))
+        def _():
+            plane_rest(n_line, {"px": 0}).wait_send()
+
+        @pl.when(me == 0)
+        def _():
+            n_recv[pl.ds(0, PY)] = n_line[...]
+            plane_rest(n_recv.at[pl.ds(PY, DEV - PY)], {"px": 1}).wait_recv()
+            for t in range(QUAD):
+                v_table[t] = n_recv[:, t, :].T
+
     column = (col_ref[0], col_ref[1])
     row = (row_ref[0], row_ref[1])
     for f in range(2):
         landed(ahead_send.at[f], ahead_recv.at[f], 8, 1 + f)
+        if f == 1:
+            last_table()
         plane = [
             jnp.concatenate(
                 [ahead_recv[f, pl.ds(c * QUAD + t, L, stride=8), :] for t in range(QUAD)], 1
@@ -298,30 +332,67 @@
         for c in range(2):
             for t in range(QUAD):
                 back_send[f, pl.ds(c * QUAD + t, L, stride=8), :] = plane[tile(c), tile(t)]
-        spread(back_send.at[f], back_recv.at[f], 8, 3 + f)
-
-    for f in range(2):
-        landed(back_send.at[f], back_recv.at[f], 8, 3 + f)
-
-    def slot(f, c):
-        rows = [back_recv[f, pl.ds(c * QUAD + t, L, stride=8), :] for t in range(QUAD)]
-        return jnp.concatenate(rows, 1)
+        if f == 0:
+            pl.when(me != 0)(lambda: spread(back_send.at[0], back_recv.at[0], 8, 3, SHIFTS))
+        else:
+
+            @pl.when(me == 0)
+            def _():
+                for t in range(QUAD):
+                    first, second = pl.ds(QUAD + t, L, stride=8), pl.ds(t, L, stride=8)
+                    held = back_send[0, first, :], back_send[1, second, :]
+                    back_send[0, first, :], back_send[1, second, :] = held[1], held[0]
+                spread(back_send.at[0], back_recv.at[0], 8, 3, SHIFTS)
+
+            spread(back_send.at[1], back_recv.at[1], 8, 4, SHIFTS)
 
     for index in range(7, 10):
         fetches[index].wait()
-    middle = (slot(0, 1), slot(1, 0))
-    imag_zero = jnp.where(at_zero, middle[1], middle[0])
-    real_one = jnp.where(at_zero, middle[0], middle[1])
-    members = ((slot(0, 0), imag_zero), (real_one, slot(1, 1)))
     zb = (zb_ref[0], zb_ref[1])
 
     def fold(start, rows):
         for h in range(2):
             half_y[h, pl.ds(start, rows.shape[0]), :] = rows[:, tile(h)]
 
-    for f in range(2):
-        cells = right_table(jnp.concatenate(members[f], 0), zb, ((0,), (0,)))
+    def pair_rows(start, count):
+        rows = [
+            half_y[h, pl.ds(start, count, stride=2), :] + half_y[h, pl.ds(start + 1, count, stride=2), :]
+            for h in range(2)
+        ]
+        return jnp.concatenate(rows, 1)
+
+    def z_pool(values, lanes):
+        high, low = parts(values)
+        pool = pool_ref[:, lanes]
+        return product(high, pool, ((1,), (0,))) + product(low, pool, ((1,), (0,)))
+
+    def across(send, recv, slot):
+        copies = [pltpu.make_async_copy(send.at[my_py], recv.at[my_py], local_sems.at[slot])]
+        for dx, low in LINE:
+            other = (((my_py >> 2) + dx) & 3) * 4 + ((my_py & 3) ^ low)
+            copies.append(
+                pltpu.make_async_remote_copy(
+                    src_ref=send.at[other],
+                    dst_ref=recv.at[my_py],
+                    send_sem=send_sems.at[slot + len(copies)],
+                    recv_sem=recv_sems.at[slot + len(copies)],
+                    device_id={"py": other},
+                    device_id_type=MESH,
+                )
+            )
+        for copy in copies:
+            copy.start()
+        return copies
+
+    def coarse(f):
+        tiles = [
+            [back_recv[f, pl.ds(c * QUAD + t, L, stride=8), :] for t in range(QUAD)]
+            for c in range(2)
+        ]
+        waves = jnp.concatenate([jnp.concatenate(part, 1) for part in tiles], 0)
+        cells = right_table(waves, zb, ((0,), (0,)))
         cells = jnp.exp(0.5 * cells)
+        start = f * 4 * CY * 2
         for t in range(QUAD):
             xs, ys = quarter(t)
             block = cells[tile(t)].reshape(8, 16, LZ)
@@ -329,70 +400,86 @@
             half_x = block.reshape(4, 2, 16, LZ)
             half_x = half_x[:, 0] + half_x[:, 1]
             for x in range(4):
-                fold(((f * 2 + t // 2) * 4 + x) * CY + (t % 2) * 16, half_x[x])
-
-    def pair_rows(count):
-        rows = [
-            half_y[h, pl.ds(0, count, stride=2), :] + half_y[h, pl.ds(1, count, stride=2), :]
-            for h in range(2)
-        ]
-        return jnp.concatenate(rows, 1)
-
-    def z_pool(values, lanes):
-        high, low = parts(values)
-        pool = pool_ref[:, lanes]
-        return product(high, pool, ((1,), (0,))) + product(low, pool, ((1,), (0,)))
-
-    rows_one = pair_rows(2 * 8 * 16)
-    one = z_pool(rows_one, slice(0, 128))
+                fold(start + ((t // 2) * 4 + x) * CY + (t % 2) * 16, half_x[x])
+        stored = pltpu.make_async_copy(mod_ref.at[f], mod_out.at[f], fetch_sems.at[len(fetches) + f])
+        stored.start()
+        rows_one = pair_rows(start, 8 * 16)
+        one = z_pool(rows_one, slice(0, 128))
+        for i in range(PY):
+            one_send[f, i] = one[i * 8 : i * 8 + 8]
+        return stored, rows_one, across(one_send.at[f], (one_recv_0, one_recv_1)[f], 7 + f * PY)
+
+    def choose(source, target, pieces):
+        for g in range(PY):
+            for level, rows in pieces:
+                target[g, rows, :] = source[group_ref[level, g], rows, :]
+
+    landed(back_send.at[0], back_recv.at[0], 8, 3)
+    stored_0, rows_0, one_0 = coarse(0)
+    landed(back_send.at[1], back_recv.at[1], 8, 4)
+    stored_1, rows_1, one_1 = coarse(1)
+    rows_one = jnp.concatenate([rows_0, rows_1], 0)
     pairs = rows_one.reshape(2 * 4, 2, 16, LZ)
     fold(0, (pairs[:, 0] + pairs[:, 1]).reshape(2 * 4 * 16, LZ))
-    rows_two = pair_rows(2 * 4 * 8)
+    rows_two = pair_rows(0, 2 * 4 * 8)
     pairs = rows_two.reshape(2 * 2, 2, 8, LZ)
     fold(0, (pairs[:, 0] + pairs[:, 1]).reshape(2 * 2 * 8, LZ))
-    rows_three = pair_rows(2 * 2 * 4)
+    rows_three = pair_rows(0, 2 * 2 * 4)
     rest = z_pool(jnp.concatenate([rows_two, rows_three], 0), slice(128, 256))
     for i in range(PY):
-        c_send[i, pl.ds(0, 16), :] = one[i * 16 : i * 16 + 16]
-        c_send[i, pl.ds(16, 4), :] = rest[i * 4 : i * 4 + 4]
-        c_send[i, pl.ds(20, 1), :] = rest[64 + i : 65 + i]
-        c_send[i, pl.ds(21, 3), :] = jnp.zeros((3, L), F32)
-
-    def across(send, recv, slot):
-        copies = [pltpu.make_async_copy(send.at[my_py], recv.at[my_py], local_sems.at[slot])]
-        for away in range(1, PY):
-            other = lax.rem(my_py + away, PY)
-            copies.append(
-                pltpu.make_async_remote_copy(
-                    src_ref=send.at[other],
-                    dst_ref=recv.at[my_py],
-                    send_sem=send_sems.at[slot + away],
-                    recv_sem=recv_sems.at[slot + away],
-                    device_id={"py": other},
-                    device_id_type=MESH,
-                )
-            )
-        for copy in copies:
-            copy.start()
-        for copy in copies:
-            copy.wait()
-
-    across(c_send, c_recv, 6)
-    for g in range(PY):
-        for level, rows in enumerate((pl.ds(0, 16), pl.ds(16, 4), pl.ds(20, 1))):
-            d_send[g, rows, :] = c_recv[group_ref[level, g], rows, :]
-        d_send[g, pl.ds(21, 3), :] = jnp.zeros((3, L), F32)
-    across(d_send, d_recv, 6 + PY)
+        rest_send[i, pl.ds(0, 4), :] = rest[i * 4 : i * 4 + 4]
+        rest_send[i, pl.ds(4, 1), :] = rest[64 + i : 65 + i]
+        rest_send[i, pl.ds(5, 3), :] = jnp.zeros((3, L), F32)
+        rest_back[i, pl.ds(5, 3), :] = jnp.zeros((3, L), F32)
+    rest_0 = across(rest_send, rest_recv, 7 + 2 * PY)
+    for copy in one_0:
+        copy.wait()
+    choose(one_recv_0, one_back.at[0], [(0, pl.ds(0, 8))])
+    last = across(one_back.at[0], one_out.at[0], 7 + 3 * PY)
+    for copy in one_1:
+        copy.wait()
+    choose(one_recv_1, one_back.at[1], [(0, pl.ds(0, 8))])
+    last += across(one_back.at[1], one_out.at[1], 7 + 4 * PY)
+    for copy in rest_0:
+        copy.wait()
+    choose(rest_recv, rest_back, [(1, pl.ds(0, 4)), (2, pl.ds(4, 1))])
+    last += across(rest_back, rest_out, 7 + 5 * PY)
+    for copy in last:
+        copy.wait()
+    stored_0.wait()
+    stored_1.wait()
+
+
+def store_kernel(
+    mod_in, one_in, rest_in, mod_out, one_out, two_out, three_out,
+    mod_ref, one_held, rest_held, one_ref, two_ref, three_ref, in_sems, out_sems,
+):
+    pairs = [(mod_in.at[f, pl.ds(h * 8, 8)], mod_ref.at[f, pl.ds(h * 8, 8)]) for f in range(2) for h in range(2)]
+    pairs += [(one_in, one_held), (rest_in, rest_held)]
+    outs = [(mod_ref.at[f, pl.ds(h * 8, 8)], mod_out.at[f, pl.ds(h * 8, 8)]) for f in range(2) for h in range(2)]
+    outs += [(one_ref, one_out), (two_ref, two_out), (three_ref, three_out)]
+    loads = [pltpu.make_async_copy(*pair, in_sems.at[i]) for i, pair in enumerate(pairs)]
+    stores = [pltpu.make_async_copy(*pair, out_sems.at[i]) for i, pair in enumerate(outs)]
+    for load in loads[4:] + loads[:4]:
+        load.start()
+    loads[4].wait()
+    loads[5].wait()
     for f in range(2):
-        for x in range(8):
-            one_ref[f, x] = d_recv[f * 8 + x, pl.ds(0, 16), :]
+        one_ref[f] = one_held[f].reshape(8, 16, L)
         for x in range(4):
             for h in range(2):
-                i = (f * 4 + x) * 2 + h
-                two_ref[f, x, pl.ds(h * 4, 4), :] = d_recv[i, pl.ds(16, 4), :][:, :64]
+                two_ref[f, x, pl.ds(h * 4, 4), :] = rest_held[(f * 4 + x) * 2 + h, pl.ds(0, 4), :][:, :64]
         for x in range(2):
             for y in range(4):
-                three_ref[f, x, pl.ds(y, 1), :] = d_recv[(f * 2 + x) * 4 + y, pl.ds(20, 1), :][:, 64:96]
+                row = rest_held[(f * 2 + x) * 4 + y, pl.ds(4, 1), :]
+                three_ref[f, x, pl.ds(y, 1), :] = row[:, 64:96]
+    for store in stores[4:]:
+        store.start()
+    for i in range(4):
+        loads[i].wait()
+        stores[i].start()
+    for store in stores:
+        store.wait()
 
 
 def on_device(white_noise, spectrum, group_table):
@@ -402,32 +489,39 @@
         (2, CX // 4, CY // 4, LZ // 4),
         (2, CX // 8, CY // 8, LZ // 8),
     ]
-    vmem = pl.BlockSpec(memory_space=pltpu.VMEM)
     hbm = pl.BlockSpec(memory_space=pltpu.HBM)
     wide = pltpu.VMEM((2, DEV * 8, L), F32)
     thin = pltpu.VMEM((DEV * QUAD, L), F32)
-    coarse = pltpu.VMEM((PY, HEIGHT, L), F32)
-    slots = 6 + 2 * PY
+    table = pltpu.VMEM((QUAD, L, L), F32)
+    one, rest = (2, PY, 8, L), (PY, 8, L)
+    slots = 7 + 6 * PY
     operands = [white_noise, spectrum] + tables()
-    return pl.pallas_call(
+    results = pl.pallas_call(
         kernel,
-        out_shape=[jax.ShapeDtypeStruct(shape, F32) for shape in shapes],
+        out_shape=[jax.ShapeDtypeStruct(shape, F32) for shape in (shapes[0], one, rest)],
         in_specs=[hbm] * (len(operands) + 1),
-        out_specs=[vmem] * 4,
+        out_specs=[hbm] * 3,
         scratch_shapes=[pltpu.SMEM(group_table.shape, jnp.int32)]
         + [pltpu.VMEM(value.shape, value.dtype) for value in operands]
-        + [
-            thin, thin, pltpu.VMEM((QUAD, L), F32), pltpu.VMEM((DEV, QUAD, L), F32),
-            pltpu.VMEM((QUAD, L, L), F32), pltpu.VMEM((QUAD, L, L), F32),
-            wide, wide, wide, wide,
-            pltpu.VMEM((2, 2 * 8 * CY, L), F32), coarse, coarse, coarse, coarse,
-            pltpu.SemaphoreType.REGULAR, pltpu.SemaphoreType.DMA((len(operands) + 1,)), pltpu.SemaphoreType.DMA((slots,)), pltpu.SemaphoreType.DMA((slots,)),
-            pltpu.SemaphoreType.DMA((slots,)),
-        ],
+        + [thin, thin, pltpu.VMEM((QUAD, L), F32)]
+        + [pltpu.VMEM((size, QUAD, L), F32) for size in (PY, DEV)]
+        + [table, table, wide, wide, wide, wide]
+        + [pltpu.VMEM(shapes[0], F32), pltpu.VMEM((2, 2 * 8 * CY, L), F32)]
+        + [pltpu.VMEM(shape, F32) for shape in (one, rest, rest, one, rest, rest, rest)]
+        + [pltpu.SemaphoreType.DMA((size,)) for size in (len(operands) + 3, slots, slots, slots)],
         compiler_params=pltpu.CompilerParams(
             collective_id=0, has_side_effects=True, vmem_limit_bytes=67_043_328
         ),
     )(group_table, *operands)
+    return pl.pallas_call(
+        store_kernel,
+        out_shape=[jax.ShapeDtypeStruct(shape, F32) for shape in shapes],
+        in_specs=[hbm] * 3,
+        out_specs=[hbm] * 4,
+        scratch_shapes=[pltpu.VMEM(shape, F32) for shape in (shapes[0], one, rest, *shapes[1:])]
+        + [pltpu.SemaphoreType.DMA((8,)), pltpu.SemaphoreType.DMA((8,))],
+        compiler_params=pltpu.CompilerParams(vmem_limit_bytes=67_043_328),
+    )(*results)
 
 
 def solution(mesh):

time: 61.6 us -> 57.2 us (0.929)
  local copies, waits for them, and re-layouts: 4.41 us -> 0 us
    unnamed x10 -> x0, local copies, waits for them, and re-layouts: 4.41 us -> none
    pallas_call x0 -> x1, Pallas kernels: none -> 2.16 us  [on_device(): pl.pallas_call(store_kernel, out_shape=[jax.ShapeDtypeStruct(shape, F32)...]
    pallas_call x1, Pallas kernels: 56.3 us -> 54.3 us  [on_device(): pl.pallas_call(kernel, out_shape=[jax.ShapeDtypeStruct(shape, F32) for sh...]
where the time goes in v3:
time: 57.2 us; the launch traced here: 57.1 us
  Pallas kernels  56.4 us (99%)
  between operations  0.64 us (1%)
    pallas_call x1, Pallas kernels, on_device(): pl.pallas_call(kernel, out_shape=[jax.ShapeDtypeStruct(shape, F32) for sh...  54.3 us
    pallas_call x1, Pallas kernels, on_device(): pl.pallas_call(store_kernel, out_shape=[jax.ShapeDtypeStruct(shape, F32)...  2.16 us

profile of v3, /device:TPU:1, one launch (start us, length us, event | category | flops | bytes accessed | tf_op | source)
XLA Modules:
  0.0 57.1 jit_solution(2380946020792896808)
XLA Ops:
  0.6 54.3 %shard_map.129 = (f32[2,16,32,256]{3,2,1,0:T(8,128)}, f32[2,16,8,128]{3,2,1,0:T(8,128)}, f32[16,8,128]{2,1,0:T(8,128)}) custom-call(s32[3,16]{1,0:T(4,128)} %group_in.1, f32[2,16,32,256]{3,2,1,0:T(8,128)} %noise_in.1, f32[16,32,256]{2,1,0:T(8,128)} %spec_in.1, bf16[2,256,256]{2,1,0:T(8,128)(2,1)} %constant.14.clone.za_in, ...), custom_call_target="tpu_custom_call" | custom-call | tf_op jit(solution)/shard_map/pallas_call | solution.py:499
  54.9 2.2 %shard_map.130 = (f32[2,16,32,256]{3,2,1,0:T(8,128)}, f32[2,8,16,128]{3,2,1,0:T(8,128)}, f32[2,4,8,64]{3,2,1,0:T(8,128)}, f32[2,2,4,32]{3,2,1,0:T(4,128)}) custom-call(f32[2,16,32,256]{3,2,1,0:T(8,128)} %get-tuple-element.7.mod_in, f32[2,16,8,128]{3,2,1,0:T(8,128)} %get-tuple-element.8.one_in, f32[16,8,128]{2,1,0:T(8,128)} %get-tuple-element.9.rest_in), custom_call_target="tpu_custom_call" | custom-call | tf_op jit(solution)/shard_map/pallas_call | solution.py:516

commit v4 on v3

--- a/solution.py
+++ b/solution.py
@@ -367,22 +367,28 @@
         return product(high, pool, ((1,), (0,))) + product(low, pool, ((1,), (0,)))
 
     def across(send, recv, slot):
-        copies = [pltpu.make_async_copy(send.at[my_py], recv.at[my_py], local_sems.at[slot])]
+        own = pltpu.make_async_copy(send.at[my_py], recv.at[my_py], local_sems.at[slot])
+        own.start()
         for dx, low in LINE:
             other = (((my_py >> 2) + dx) & 3) * 4 + ((my_py & 3) ^ low)
-            copies.append(
-                pltpu.make_async_remote_copy(
-                    src_ref=send.at[other],
-                    dst_ref=recv.at[my_py],
-                    send_sem=send_sems.at[slot + len(copies)],
-                    recv_sem=recv_sems.at[slot + len(copies)],
-                    device_id={"py": other},
-                    device_id_type=MESH,
-                )
-            )
-        for copy in copies:
-            copy.start()
-        return copies
+            pltpu.make_async_remote_copy(
+                src_ref=send.at[other],
+                dst_ref=recv.at[my_py],
+                send_sem=send_sems.at[slot],
+                recv_sem=recv_sems.at[slot],
+                device_id={"py": other},
+                device_id_type=MESH,
+            ).start()
+        rest = pl.ds(0, PY - 1)
+        whole = pltpu.make_async_remote_copy(
+            src_ref=send.at[rest],
+            dst_ref=recv.at[rest],
+            send_sem=send_sems.at[slot],
+            recv_sem=recv_sems.at[slot],
+            device_id={"py": my_py ^ 1},
+            device_id_type=MESH,
+        )
+        return [own, whole]
 
     def coarse(f):
         tiles = [
@@ -407,7 +413,7 @@
         one = z_pool(rows_one, slice(0, 128))
         for i in range(PY):
             one_send[f, i] = one[i * 8 : i * 8 + 8]
-        return stored, rows_one, across(one_send.at[f], (one_recv_0, one_recv_1)[f], 7 + f * PY)
+        return stored, rows_one, across(one_send.at[f], (one_recv_0, one_recv_1)[f], 7 + f)
 
     def choose(source, target, pieces):
         for g in range(PY):
@@ -431,19 +437,19 @@
         rest_send[i, pl.ds(4, 1), :] = rest[64 + i : 65 + i]
         rest_send[i, pl.ds(5, 3), :] = jnp.zeros((3, L), F32)
         rest_back[i, pl.ds(5, 3), :] = jnp.zeros((3, L), F32)
-    rest_0 = across(rest_send, rest_recv, 7 + 2 * PY)
+    rest_0 = across(rest_send, rest_recv, 9)
     for copy in one_0:
         copy.wait()
     choose(one_recv_0, one_back.at[0], [(0, pl.ds(0, 8))])
-    last = across(one_back.at[0], one_out.at[0], 7 + 3 * PY)
+    last = across(one_back.at[0], one_out.at[0], 10)
     for copy in one_1:
         copy.wait()
     choose(one_recv_1, one_back.at[1], [(0, pl.ds(0, 8))])
-    last += across(one_back.at[1], one_out.at[1], 7 + 4 * PY)
+    last += across(one_back.at[1], one_out.at[1], 11)
     for copy in rest_0:
         copy.wait()
     choose(rest_recv, rest_back, [(1, pl.ds(0, 4)), (2, pl.ds(4, 1))])
-    last += across(rest_back, rest_out, 7 + 5 * PY)
+    last += across(rest_back, rest_out, 12)
     for copy in last:
         copy.wait()
     stored_0.wait()
@@ -494,7 +500,7 @@
     thin = pltpu.VMEM((DEV * QUAD, L), F32)
     table = pltpu.VMEM((QUAD, L, L), F32)
     one, rest = (2, PY, 8, L), (PY, 8, L)
-    slots = 7 + 6 * PY
+    slots = 13
     operands = [white_noise, spectrum] + tables()
     results = pl.pallas_call(
         kernel,

time: 57.2 us -> 54.7 us (0.956)
  Pallas kernels: 56.4 us -> 53.9 us
    pallas_call x1, Pallas kernels: 54.3 us -> 51.8 us  [on_device(): pl.pallas_call(kernel, out_shape=[jax.ShapeDtypeStruct(shape, F32) for sh...]
where the time goes in v4:
time: 54.7 us; the launch traced here: 54.6 us
  Pallas kernels  53.9 us (99%)
  between operations  0.64 us (1%)
    pallas_call x1, Pallas kernels, on_device(): pl.pallas_call(kernel, out_shape=[jax.ShapeDtypeStruct(shape, F32) for sh...  51.8 us
    pallas_call x1, Pallas kernels, on_device(): pl.pallas_call(store_kernel, out_shape=[jax.ShapeDtypeStruct(shape, F32)...  2.16 us

profile of v4, /device:TPU:1, one launch (start us, length us, event | category | flops | bytes accessed | tf_op | source)
XLA Modules:
  0.0 54.6 jit_solution(6212415394585138522)
XLA Ops:
  0.6 51.8 %shard_map.129 = (f32[2,16,32,256]{3,2,1,0:T(8,128)}, f32[2,16,8,128]{3,2,1,0:T(8,128)}, f32[16,8,128]{2,1,0:T(8,128)}) custom-call(s32[3,16]{1,0:T(4,128)} %group_in.1, f32[2,16,32,256]{3,2,1,0:T(8,128)} %noise_in.1, f32[16,32,256]{2,1,0:T(8,128)} %spec_in.1, bf16[2,256,256]{2,1,0:T(8,128)(2,1)} %constant.14.clone.za_in, ...), custom_call_target="tpu_custom_call" | custom-call | tf_op jit(solution)/shard_map/pallas_call | solution.py:505
  52.4 2.2 %shard_map.130 = (f32[2,16,32,256]{3,2,1,0:T(8,128)}, f32[2,8,16,128]{3,2,1,0:T(8,128)}, f32[2,4,8,64]{3,2,1,0:T(8,128)}, f32[2,2,4,32]{3,2,1,0:T(4,128)}) custom-call(f32[2,16,32,256]{3,2,1,0:T(8,128)} %get-tuple-element.7.mod_in, f32[2,16,8,128]{3,2,1,0:T(8,128)} %get-tuple-element.8.one_in, f32[16,8,128]{2,1,0:T(8,128)} %get-tuple-element.9.rest_in), custom_call_target="tpu_custom_call" | custom-call | tf_op jit(solution)/shard_map/pallas_call | solution.py:522

commit v5 on v4

--- a/solution.py
+++ b/solution.py
@@ -87,7 +87,28 @@
 
 
 SHIFTS = [(dz, dy, dx, dc) for dz in range(4) for dy in range(4) for dx in range(4) for dc in range(2)]
-MIXED = [SHIFTS[(i * 37) % 128] for i in range(1, 128)]
+
+
+def spread_evenly(shifts):
+    load = np.zeros(6)
+    order, left = [], list(shifts)
+    while left:
+        def cost(shift):
+            after = load.copy()
+            for axis, d in enumerate(shift[:3]):
+                after[2 * axis] += (0, 1, 1, 0)[d]
+                after[2 * axis + 1] += (0, 0, 1, 1)[d]
+            return after.max() - after.min()
+        best = min(left, key=cost)
+        for axis, d in enumerate(best[:3]):
+            load[2 * axis] += (0, 1, 1, 0)[d]
+            load[2 * axis + 1] += (0, 0, 1, 1)[d]
+        left.remove(best)
+        order.append(best)
+    return order
+
+
+MIXED = spread_evenly([SHIFTS[(i * 37) % 128] for i in range(1, 128)])
 SHIFTS = sorted(SHIFTS[1:], key=lambda shift: -hops(shift))
 
 LINE = [(dx, low) for dx in range(4) for low in range(4)]
@@ -132,7 +153,7 @@
     group_in, noise_in, spec_in, za_in, zb_in, col_in, row_in, tw_in, small_in, pool_in,
     mod_out, one_out, rest_out,
     group_ref, noise_ref, spec_ref, za_ref, zb_ref, col_ref, row_ref, tw_ref, small_ref, pool_ref,
-    s_send, s_recv, n_send, n_line, n_recv, u_table, v_table, ahead_send, ahead_recv, back_send, back_recv,
+    s_send, s_recv, n_send, n_line, n_recv, u_table, v_table, ahead_send, ahead_recv, back_send, back_recv, zero_send,
     mod_ref, half_y, one_send, one_recv_0, one_recv_1, one_back, rest_send, rest_recv, rest_back,
     fetch_sems, local_sems, send_sems, recv_sems,
 ):
@@ -175,10 +196,14 @@
         for shift in order:
             send_to(shift)
 
-    def landed(send, recv, height, slot):
-        pltpu.make_async_copy(
+    def landed(send, recv, height, slot, packed=False):
+        own = pltpu.make_async_copy(
             send.at[piece(me, height)], recv.at[piece(me, height)], local_sems.at[slot]
-        ).wait()
+        )
+        if packed:
+            pl.when(me != 0)(own.wait)
+        else:
+            own.wait()
         rest = pl.ds(0, (DEV - 1) * height)
         whole = pltpu.make_async_remote_copy(
             src_ref=send.at[rest],
@@ -264,7 +289,7 @@
             for copy in plane_copies:
                 copy.start()
 
-    spread(ahead_send.at[1], ahead_recv.at[1], 8, 2)
+    spread(ahead_send.at[1], ahead_recv.at[1], 8, 2, SHIFTS)
 
     landed(s_send, s_recv, QUAD, 0)
     for t in range(QUAD):
@@ -329,22 +354,39 @@
         imag = jnp.concatenate(butterfly(imags), 1)
         real, imag = turned(real, imag, tw_ref[0], -tw_ref[1])
         plane = left_table(row, jnp.concatenate([real, imag], 0))
-        for c in range(2):
-            for t in range(QUAD):
-                back_send[f, pl.ds(c * QUAD + t, L, stride=8), :] = plane[tile(c), tile(t)]
-        if f == 0:
-            pl.when(me != 0)(lambda: spread(back_send.at[0], back_recv.at[0], 8, 3, SHIFTS))
-        else:
-
-            @pl.when(me == 0)
-            def _():
+        @pl.when(me != 0)
+        def _():
+            for c in range(2):
                 for t in range(QUAD):
-                    first, second = pl.ds(QUAD + t, L, stride=8), pl.ds(t, L, stride=8)
-                    held = back_send[0, first, :], back_send[1, second, :]
-                    back_send[0, first, :], back_send[1, second, :] = held[1], held[0]
-                spread(back_send.at[0], back_recv.at[0], 8, 3, SHIFTS)
-
-            spread(back_send.at[1], back_recv.at[1], 8, 4, SHIFTS)
+                    back_send[f, pl.ds(c * QUAD + t, L, stride=8), :] = plane[tile(c), tile(t)]
+            spread(back_send.at[f], back_recv.at[f], 8, 3 + f, SHIFTS)
+
+        @pl.when(me == 0)
+        def _():
+            for c in range(2):
+                for t in range(QUAD):
+                    zero_send[f, c, pl.ds(t, L, stride=QUAD), :] = plane[tile(c), tile(t)]
+                back_recv[c, pl.ds(f * QUAD, QUAD), :] = zero_send[f, c, pl.ds(0, QUAD), :]
+
+            def send_to(shift):
+                other, device = shifted(here, *shift)
+                for c in range(2):
+                    pltpu.make_async_remote_copy(
+                        src_ref=zero_send.at[f, c, piece(other, QUAD)],
+                        dst_ref=back_recv.at[c, pl.ds(f * QUAD, QUAD)],
+                        send_sem=send_sems.at[3 + c],
+                        recv_sem=recv_sems.at[3 + c],
+                        device_id=device,
+                        device_id_type=MESH,
+                    ).start()
+
+            @pl.loop(0, 16)
+            def _(step):
+                dx, dy = step & 3, step >> 2
+                pl.when(step != 0)(lambda: send_to((0, dy, dx, 0)))
+                for n in range(1, 8):
+                    dz, dc = n >> 1, n & 1
+                    send_to((dz, dy + n, dx + dz, dc))
 
     for index in range(7, 10):
         fetches[index].wait()
@@ -420,9 +462,9 @@
             for level, rows in pieces:
                 target[g, rows, :] = source[group_ref[level, g], rows, :]
 
-    landed(back_send.at[0], back_recv.at[0], 8, 3)
+    landed(back_send.at[0], back_recv.at[0], 8, 3, True)
     stored_0, rows_0, one_0 = coarse(0)
-    landed(back_send.at[1], back_recv.at[1], 8, 4)
+    landed(back_send.at[1], back_recv.at[1], 8, 4, True)
     stored_1, rows_1, one_1 = coarse(1)
     rows_one = jnp.concatenate([rows_0, rows_1], 0)
     pairs = rows_one.reshape(2 * 4, 2, 16, LZ)
@@ -511,7 +553,7 @@
         + [pltpu.VMEM(value.shape, value.dtype) for value in operands]
         + [thin, thin, pltpu.VMEM((QUAD, L), F32)]
         + [pltpu.VMEM((size, QUAD, L), F32) for size in (PY, DEV)]
-        + [table, table, wide, wide, wide, wide]
+        + [table, table, wide, wide, wide, wide, pltpu.VMEM((2, 2, DEV * QUAD, L), F32)]
         + [pltpu.VMEM(shapes[0], F32), pltpu.VMEM((2, 2 * 8 * CY, L), F32)]
         + [pltpu.VMEM(shape, F32) for shape in (one, rest, rest, one, rest, rest, rest)]
         + [pltpu.SemaphoreType.DMA((size,)) for size in (len(operands) + 3, slots, slots, slots)],

time: 54.7 us -> 52.9 us (0.967)
  Pallas kernels: 53.9 us -> 52.1 us
    pallas_call x1, Pallas kernels: 51.8 us -> 50 us  [on_device(): pl.pallas_call(kernel, out_shape=[jax.ShapeDtypeStruct(shape, F32) for sh...]
where the time goes in v5:
time: 52.9 us; the launch traced here: 52.8 us
  Pallas kernels  52.1 us (98%)
  between operations  0.64 us (1%)
    pallas_call x1, Pallas kernels, on_device(): pl.pallas_call(kernel, out_shape=[jax.ShapeDtypeStruct(shape, F32) for sh...  50 us
    pallas_call x1, Pallas kernels, on_device(): pl.pallas_call(store_kernel, out_shape=[jax.ShapeDtypeStruct(shape, F32)...  2.16 us

profile of v5, /device:TPU:1, one launch (start us, length us, event | category | flops | bytes accessed | tf_op | source)
XLA Modules:
  0.0 52.8 jit_solution(9147849795104430801)
XLA Ops:
  0.6 50.0 %shard_map.129 = (f32[2,16,32,256]{3,2,1,0:T(8,128)}, f32[2,16,8,128]{3,2,1,0:T(8,128)}, f32[16,8,128]{2,1,0:T(8,128)}) custom-call(s32[3,16]{1,0:T(4,128)} %group_in.1, f32[2,16,32,256]{3,2,1,0:T(8,128)} %noise_in.1, f32[16,32,256]{2,1,0:T(8,128)} %spec_in.1, bf16[2,256,256]{2,1,0:T(8,128)(2,1)} %constant.14.clone.za_in, ...), custom_call_target="tpu_custom_call" | custom-call | tf_op jit(solution)/shard_map/pallas_call | solution.py:547
  50.6 2.2 %shard_map.130 = (f32[2,16,32,256]{3,2,1,0:T(8,128)}, f32[2,8,16,128]{3,2,1,0:T(8,128)}, f32[2,4,8,64]{3,2,1,0:T(8,128)}, f32[2,2,4,32]{3,2,1,0:T(4,128)}) custom-call(f32[2,16,32,256]{3,2,1,0:T(8,128)} %get-tuple-element.7.mod_in, f32[2,16,8,128]{3,2,1,0:T(8,128)} %get-tuple-element.8.one_in, f32[16,8,128]{2,1,0:T(8,128)} %get-tuple-element.9.rest_in), custom_call_target="tpu_custom_call" | custom-call | tf_op jit(solution)/shard_map/pallas_call | solution.py:564

commit v6 on v5

--- a/solution.py
+++ b/solution.py
@@ -154,7 +154,7 @@
     mod_out, one_out, rest_out,
     group_ref, noise_ref, spec_ref, za_ref, zb_ref, col_ref, row_ref, tw_ref, small_ref, pool_ref,
     s_send, s_recv, n_send, n_line, n_recv, u_table, v_table, ahead_send, ahead_recv, back_send, back_recv, zero_send,
-    mod_ref, half_y, one_send, one_recv_0, one_recv_1, one_back, rest_send, rest_recv, rest_back,
+    half_y, one_send, one_recv_0, one_recv_1, one_back, rest_send, rest_recv, rest_back,
     fetch_sems, local_sems, send_sems, recv_sems,
 ):
     here = place()
@@ -444,18 +444,16 @@
         for t in range(QUAD):
             xs, ys = quarter(t)
             block = cells[tile(t)].reshape(8, 16, LZ)
-            mod_ref[f, xs, ys, :] = block
+            mod_out[f, xs, ys, :] = block
             half_x = block.reshape(4, 2, 16, LZ)
             half_x = half_x[:, 0] + half_x[:, 1]
             for x in range(4):
                 fold(start + ((t // 2) * 4 + x) * CY + (t % 2) * 16, half_x[x])
-        stored = pltpu.make_async_copy(mod_ref.at[f], mod_out.at[f], fetch_sems.at[len(fetches) + f])
-        stored.start()
         rows_one = pair_rows(start, 8 * 16)
         one = z_pool(rows_one, slice(0, 128))
         for i in range(PY):
             one_send[f, i] = one[i * 8 : i * 8 + 8]
-        return stored, rows_one, across(one_send.at[f], (one_recv_0, one_recv_1)[f], 7 + f)
+        return rows_one, across(one_send.at[f], (one_recv_0, one_recv_1)[f], 7 + f)
 
     def choose(source, target, pieces):
         for g in range(PY):
@@ -463,9 +461,9 @@
                 target[g, rows, :] = source[group_ref[level, g], rows, :]
 
     landed(back_send.at[0], back_recv.at[0], 8, 3, True)
-    stored_0, rows_0, one_0 = coarse(0)
+    rows_0, one_0 = coarse(0)
     landed(back_send.at[1], back_recv.at[1], 8, 4, True)
-    stored_1, rows_1, one_1 = coarse(1)
+    rows_1, one_1 = coarse(1)
     rows_one = jnp.concatenate([rows_0, rows_1], 0)
     pairs = rows_one.reshape(2 * 4, 2, 16, LZ)
     fold(0, (pairs[:, 0] + pairs[:, 1]).reshape(2 * 4 * 16, LZ))
@@ -494,38 +492,25 @@
     last += across(rest_back, rest_out, 12)
     for copy in last:
         copy.wait()
-    stored_0.wait()
-    stored_1.wait()
 
 
 def store_kernel(
-    mod_in, one_in, rest_in, mod_out, one_out, two_out, three_out,
-    mod_ref, one_held, rest_held, one_ref, two_ref, three_ref, in_sems, out_sems,
+    mod_in, one_in, rest_in, mod_out, one_out, two_out, three_out, one_ref, two_ref, three_ref, sems,
 ):
-    pairs = [(mod_in.at[f, pl.ds(h * 8, 8)], mod_ref.at[f, pl.ds(h * 8, 8)]) for f in range(2) for h in range(2)]
-    pairs += [(one_in, one_held), (rest_in, rest_held)]
-    outs = [(mod_ref.at[f, pl.ds(h * 8, 8)], mod_out.at[f, pl.ds(h * 8, 8)]) for f in range(2) for h in range(2)]
-    outs += [(one_ref, one_out), (two_ref, two_out), (three_ref, three_out)]
-    loads = [pltpu.make_async_copy(*pair, in_sems.at[i]) for i, pair in enumerate(pairs)]
-    stores = [pltpu.make_async_copy(*pair, out_sems.at[i]) for i, pair in enumerate(outs)]
-    for load in loads[4:] + loads[:4]:
-        load.start()
-    loads[4].wait()
-    loads[5].wait()
+    outs = [(mod_in, mod_out), (one_ref, one_out), (two_ref, two_out), (three_ref, three_out)]
+    stores = [pltpu.make_async_copy(*pair, sems.at[i]) for i, pair in enumerate(outs)]
+    stores[0].start()
     for f in range(2):
-        one_ref[f] = one_held[f].reshape(8, 16, L)
+        one_ref[f] = one_in[f].reshape(8, 16, L)
         for x in range(4):
             for h in range(2):
-                two_ref[f, x, pl.ds(h * 4, 4), :] = rest_held[(f * 4 + x) * 2 + h, pl.ds(0, 4), :][:, :64]
+                two_ref[f, x, pl.ds(h * 4, 4), :] = rest_in[(f * 4 + x) * 2 + h, pl.ds(0, 4), :][:, :64]
         for x in range(2):
             for y in range(4):
-                row = rest_held[(f * 2 + x) * 4 + y, pl.ds(4, 1), :]
+                row = rest_in[(f * 2 + x) * 4 + y, pl.ds(4, 1), :]
                 three_ref[f, x, pl.ds(y, 1), :] = row[:, 64:96]
-    for store in stores[4:]:
+    for store in stores[1:]:
         store.start()
-    for i in range(4):
-        loads[i].wait()
-        stores[i].start()
     for store in stores:
         store.wait()
 
@@ -548,27 +533,26 @@
         kernel,
         out_shape=[jax.ShapeDtypeStruct(shape, F32) for shape in (shapes[0], one, rest)],
         in_specs=[hbm] * (len(operands) + 1),
-        out_specs=[hbm] * 3,
+        out_specs=[pl.BlockSpec(memory_space=pltpu.VMEM)] * 3,
         scratch_shapes=[pltpu.SMEM(group_table.shape, jnp.int32)]
         + [pltpu.VMEM(value.shape, value.dtype) for value in operands]
         + [thin, thin, pltpu.VMEM((QUAD, L), F32)]
         + [pltpu.VMEM((size, QUAD, L), F32) for size in (PY, DEV)]
         + [table, table, wide, wide, wide, wide, pltpu.VMEM((2, 2, DEV * QUAD, L), F32)]
-        + [pltpu.VMEM(shapes[0], F32), pltpu.VMEM((2, 2 * 8 * CY, L), F32)]
+        + [pltpu.VMEM((2, 2 * 8 * CY, L), F32)]
         + [pltpu.VMEM(shape, F32) for shape in (one, rest, rest, one, rest, rest, rest)]
         + [pltpu.SemaphoreType.DMA((size,)) for size in (len(operands) + 3, slots, slots, slots)],
         compiler_params=pltpu.CompilerParams(
-            collective_id=0, has_side_effects=True, vmem_limit_bytes=67_043_328
+            collective_id=0, has_side_effects=True, vmem_limit_bytes=48 * 1024 * 1024
         ),
-    )(group_table, *operands)
+    )(*[pltpu.with_memory_space_constraint(v, pltpu.HBM) for v in [group_table] + operands])
     return pl.pallas_call(
         store_kernel,
         out_shape=[jax.ShapeDtypeStruct(shape, F32) for shape in shapes],
-        in_specs=[hbm] * 3,
+        in_specs=[pl.BlockSpec(memory_space=pltpu.VMEM)] * 3,
         out_specs=[hbm] * 4,
-        scratch_shapes=[pltpu.VMEM(shape, F32) for shape in (shapes[0], one, rest, *shapes[1:])]
-        + [pltpu.SemaphoreType.DMA((8,)), pltpu.SemaphoreType.DMA((8,))],
-        compiler_params=pltpu.CompilerParams(vmem_limit_bytes=67_043_328),
+        scratch_shapes=[pltpu.VMEM(shape, F32) for shape in shapes[1:]] + [pltpu.SemaphoreType.DMA((4,))],
+        compiler_params=pltpu.CompilerParams(vmem_limit_bytes=2 * 1024 * 1024),
     )(*results)
 
 

time: 52.9 us -> 51.7 us (0.977)
  Pallas kernels: 52.1 us -> 50.9 us
    pallas_call x1, Pallas kernels: 2.16 us -> 1.04 us  [on_device(): pl.pallas_call(store_kernel, out_shape=[jax.ShapeDtypeStruct(shape, F32)...]
where the time goes in v6:
time: 51.7 us; the launch traced here: 51.6 us
  Pallas kernels  50.9 us (98%)
  between operations  0.64 us (1%)
    pallas_call x1, Pallas kernels, on_device(): pl.pallas_call(kernel, out_shape=[jax.ShapeDtypeStruct(shape, F32) for sh...  49.9 us
    pallas_call x1, Pallas kernels, on_device(): pl.pallas_call(store_kernel, out_shape=[jax.ShapeDtypeStruct(shape, F32)...  1.04 us

profile of v6, /device:TPU:1, one launch (start us, length us, event | category | flops | bytes accessed | tf_op | source)
XLA Modules:
  0.0 51.6 jit_solution(12882126330149966072)
XLA Ops:
  0.6 49.9 %shard_map.129 = (f32[2,16,32,256]{3,2,1,0:T(8,128)S(1)}, f32[2,16,8,128]{3,2,1,0:T(8,128)S(1)}, f32[16,8,128]{2,1,0:T(8,128)S(1)}) custom-call(s32[3,16]{1,0:T(4,128)} %group_in.1, f32[2,16,32,256]{3,2,1,0:T(8,128)} %noise_in.1, f32[16,32,256]{2,1,0:T(8,128)} %spec_in.1, bf16[2,256,256]{2,1,0:T(8,128)(2,1)} %constant.14.clone.za_in, ...), custom_call_target="tpu_custom_call" | custom-call | tf_op jit(solution)/shard_map/pallas_call | solution.py:532
  50.5 1.0 %shard_map.130 = (f32[2,16,32,256]{3,2,1,0:T(8,128)}, f32[2,8,16,128]{3,2,1,0:T(8,128)}, f32[2,4,8,64]{3,2,1,0:T(8,128)}, f32[2,2,4,32]{3,2,1,0:T(4,128)}) custom-call(f32[2,16,32,256]{3,2,1,0:T(8,128)S(1)} %get-tuple-element.7.mod_in, f32[2,16,8,128]{3,2,1,0:T(8,128)S(1)} %get-tuple-element.8.one_in, f32[16,8,128]{2,1,0:T(8,128)S(1)} %get-tuple-element.9.rest_in), custom_call_target="tpu_custom_call" | custom-call | tf_op jit(solution)/shard_map/pallas_call | solution.py:549

commit v7 on v6

--- a/solution.py
+++ b/solution.py
@@ -155,7 +155,7 @@
     group_ref, noise_ref, spec_ref, za_ref, zb_ref, col_ref, row_ref, tw_ref, small_ref, pool_ref,
     s_send, s_recv, n_send, n_line, n_recv, u_table, v_table, ahead_send, ahead_recv, back_send, back_recv, zero_send,
     half_y, one_send, one_recv_0, one_recv_1, one_back, rest_send, rest_recv, rest_back,
-    fetch_sems, local_sems, send_sems, recv_sems,
+    own_sem, fetch_sems, send_sems, recv_sems,
 ):
     here = place()
     my_px, my_py = lax.axis_index("px"), lax.axis_index("py")
@@ -178,9 +178,10 @@
         pl.semaphore_signal(barrier, inc=1, device_id=shifted(here, *shift)[1], device_id_type=MESH)
 
     def spread(send, recv, height, slot, order=MIXED):
-        pltpu.make_async_copy(
-            send.at[piece(me, height)], recv.at[piece(me, height)], local_sems.at[slot]
-        ).start()
+        if height == QUAD:
+            pltpu.make_async_copy(send.at[piece(me, height)], recv.at[piece(me, height)], own_sem).start()
+        else:
+            recv[piece(me, height), :] = send[piece(me, height), :]
 
         def send_to(shift):
             other, device = shifted(here, *shift)
@@ -196,14 +197,9 @@
         for shift in order:
             send_to(shift)
 
-    def landed(send, recv, height, slot, packed=False):
-        own = pltpu.make_async_copy(
-            send.at[piece(me, height)], recv.at[piece(me, height)], local_sems.at[slot]
-        )
-        if packed:
-            pl.when(me != 0)(own.wait)
-        else:
-            own.wait()
+    def landed(send, recv, height, slot):
+        if height == QUAD:
+            pltpu.make_async_copy(send.at[piece(me, height)], recv.at[piece(me, height)], own_sem).wait()
         rest = pl.ds(0, (DEV - 1) * height)
         whole = pltpu.make_async_remote_copy(
             src_ref=send.at[rest],
@@ -409,8 +405,7 @@
         return product(high, pool, ((1,), (0,))) + product(low, pool, ((1,), (0,)))
 
     def across(send, recv, slot):
-        own = pltpu.make_async_copy(send.at[my_py], recv.at[my_py], local_sems.at[slot])
-        own.start()
+        recv[my_py] = send[my_py]
         for dx, low in LINE:
             other = (((my_py >> 2) + dx) & 3) * 4 + ((my_py & 3) ^ low)
             pltpu.make_async_remote_copy(
@@ -430,7 +425,7 @@
             device_id={"py": my_py ^ 1},
             device_id_type=MESH,
         )
-        return [own, whole]
+        return whole
 
     def coarse(f):
         tiles = [
@@ -453,43 +448,41 @@
         one = z_pool(rows_one, slice(0, 128))
         for i in range(PY):
             one_send[f, i] = one[i * 8 : i * 8 + 8]
-        return rows_one, across(one_send.at[f], (one_recv_0, one_recv_1)[f], 7 + f)
+        routed = across(one_send.at[f], (one_recv_0, one_recv_1)[f], 7 + f)
+        pairs = rows_one.reshape(4, 2, 16, LZ)
+        fold(start, (pairs[:, 0] + pairs[:, 1]).reshape(4 * 16, LZ))
+        rows_two = pair_rows(start, 4 * 8)
+        pairs = rows_two.reshape(2, 2, 8, LZ)
+        fold(start, (pairs[:, 0] + pairs[:, 1]).reshape(2 * 8, LZ))
+        rows_three = pair_rows(start, 2 * 4)
+        rest = z_pool(jnp.concatenate([rows_two, rows_three], 0), slice(128, 256))
+        for n in range(8):
+            i = f * 8 + n
+            rest_send[i, pl.ds(0, 4), :] = rest[n * 4 : n * 4 + 4]
+            rest_send[i, pl.ds(4, 1), :] = rest[32 + n : 33 + n]
+            rest_send[i, pl.ds(5, 3), :] = jnp.zeros((3, L), F32)
+            rest_back[i, pl.ds(5, 3), :] = jnp.zeros((3, L), F32)
+        return routed
 
     def choose(source, target, pieces):
         for g in range(PY):
             for level, rows in pieces:
                 target[g, rows, :] = source[group_ref[level, g], rows, :]
 
-    landed(back_send.at[0], back_recv.at[0], 8, 3, True)
-    rows_0, one_0 = coarse(0)
-    landed(back_send.at[1], back_recv.at[1], 8, 4, True)
-    rows_1, one_1 = coarse(1)
-    rows_one = jnp.concatenate([rows_0, rows_1], 0)
-    pairs = rows_one.reshape(2 * 4, 2, 16, LZ)
-    fold(0, (pairs[:, 0] + pairs[:, 1]).reshape(2 * 4 * 16, LZ))
-    rows_two = pair_rows(0, 2 * 4 * 8)
-    pairs = rows_two.reshape(2 * 2, 2, 8, LZ)
-    fold(0, (pairs[:, 0] + pairs[:, 1]).reshape(2 * 2 * 8, LZ))
-    rows_three = pair_rows(0, 2 * 2 * 4)
-    rest = z_pool(jnp.concatenate([rows_two, rows_three], 0), slice(128, 256))
-    for i in range(PY):
-        rest_send[i, pl.ds(0, 4), :] = rest[i * 4 : i * 4 + 4]
-        rest_send[i, pl.ds(4, 1), :] = rest[64 + i : 65 + i]
-        rest_send[i, pl.ds(5, 3), :] = jnp.zeros((3, L), F32)
-        rest_back[i, pl.ds(5, 3), :] = jnp.zeros((3, L), F32)
+    landed(back_send.at[0], back_recv.at[0], 8, 3)
+    one_0 = coarse(0)
+    landed(back_send.at[1], back_recv.at[1], 8, 4)
+    one_1 = coarse(1)
     rest_0 = across(rest_send, rest_recv, 9)
-    for copy in one_0:
-        copy.wait()
+    one_0.wait()
     choose(one_recv_0, one_back.at[0], [(0, pl.ds(0, 8))])
-    last = across(one_back.at[0], one_out.at[0], 10)
-    for copy in one_1:
-        copy.wait()
+    last = [across(one_back.at[0], one_out.at[0], 10)]
+    one_1.wait()
     choose(one_recv_1, one_back.at[1], [(0, pl.ds(0, 8))])
-    last += across(one_back.at[1], one_out.at[1], 11)
-    for copy in rest_0:
-        copy.wait()
+    last.append(across(one_back.at[1], one_out.at[1], 11))
+    rest_0.wait()
     choose(rest_recv, rest_back, [(1, pl.ds(0, 4)), (2, pl.ds(4, 1))])
-    last += across(rest_back, rest_out, 12)
+    last.append(across(rest_back, rest_out, 12))
     for copy in last:
         copy.wait()
 
@@ -541,7 +534,8 @@
         + [table, table, wide, wide, wide, wide, pltpu.VMEM((2, 2, DEV * QUAD, L), F32)]
         + [pltpu.VMEM((2, 2 * 8 * CY, L), F32)]
         + [pltpu.VMEM(shape, F32) for shape in (one, rest, rest, one, rest, rest, rest)]
-        + [pltpu.SemaphoreType.DMA((size,)) for size in (len(operands) + 3, slots, slots, slots)],
+        + [pltpu.SemaphoreType.DMA]
+        + [pltpu.SemaphoreType.DMA((size,)) for size in (len(operands) + 1, slots, slots)],
         compiler_params=pltpu.CompilerParams(
             collective_id=0, has_side_effects=True, vmem_limit_bytes=48 * 1024 * 1024
         ),

time: 51.7 us -> 51.5 us (level)
  no operation moved by 1% of the time
where the time goes in v7:
time: 51.5 us; the launch traced here: 51.4 us
  Pallas kernels  50.8 us (99%)
  between operations  0.64 us (1%)
    pallas_call x1, Pallas kernels, on_device(): pl.pallas_call(kernel, out_shape=[jax.ShapeDtypeStruct(shape, F32) for sh...  49.7 us
    pallas_call x1, Pallas kernels, on_device(): pl.pallas_call(store_kernel, out_shape=[jax.ShapeDtypeStruct(shape, F32)...  1.04 us

profile of v7, /device:TPU:1, one launch (start us, length us, event | category | flops | bytes accessed | tf_op | source)
XLA Modules:
  0.0 51.4 jit_solution(5127021044513881714)
XLA Ops:
  0.6 49.7 %shard_map.129 = (f32[2,16,32,256]{3,2,1,0:T(8,128)S(1)}, f32[2,16,8,128]{3,2,1,0:T(8,128)S(1)}, f32[16,8,128]{2,1,0:T(8,128)S(1)}) custom-call(s32[3,16]{1,0:T(4,128)} %group_in.1, f32[2,16,32,256]{3,2,1,0:T(8,128)} %noise_in.1, f32[16,32,256]{2,1,0:T(8,128)} %spec_in.1, bf16[2,256,256]{2,1,0:T(8,128)(2,1)} %constant.14.clone.za_in, ...), custom_call_target="tpu_custom_call" | custom-call | tf_op jit(solution)/shard_map/pallas_call | solution.py:525
  50.3 1.0 %shard_map.130 = (f32[2,16,32,256]{3,2,1,0:T(8,128)}, f32[2,8,16,128]{3,2,1,0:T(8,128)}, f32[2,4,8,64]{3,2,1,0:T(8,128)}, f32[2,2,4,32]{3,2,1,0:T(4,128)}) custom-call(f32[2,16,32,256]{3,2,1,0:T(8,128)S(1)} %get-tuple-element.7.mod_in, f32[2,16,8,128]{3,2,1,0:T(8,128)S(1)} %get-tuple-element.8.one_in, f32[16,8,128]{2,1,0:T(8,128)S(1)} %get-tuple-element.9.rest_in), custom_call_target="tpu_custom_call" | custom-call | tf_op jit(solution)/shard_map/pallas_call | solution.py:543

commit v8 on v7

--- a/solution.py
+++ b/solution.py
@@ -109,7 +109,7 @@
 
 
 MIXED = spread_evenly([SHIFTS[(i * 37) % 128] for i in range(1, 128)])
-SHIFTS = sorted(SHIFTS[1:], key=lambda shift: -hops(shift))
+SHIFTS = [shift for count in (6, 5, 4, 3, 2, 1, 0) for shift in spread_evenly([m for m in MIXED if hops(m) == count])]
 
 LINE = [(dx, low) for dx in range(4) for low in range(4)]
 LINE = sorted(LINE[1:], key=lambda move: -min(move[0], 4 - move[0]) - (move[1] >> 1))

time: 51.5 us -> 51.4 us (level)
  no operation moved by 1% of the time
where the time goes in v8:
time: 51.4 us; the launch traced here: 51.2 us
  Pallas kernels  50.6 us (98%)
  between operations  0.64 us (1%)
    pallas_call x1, Pallas kernels, on_device(): pl.pallas_call(kernel, out_shape=[jax.ShapeDtypeStruct(shape, F32) for sh...  49.6 us
    pallas_call x1, Pallas kernels, on_device(): pl.pallas_call(store_kernel, out_shape=[jax.ShapeDtypeStruct(shape, F32)...  1.04 us

profile of v8, /device:TPU:1, one launch (start us, length us, event | category | flops | bytes accessed | tf_op | source)
XLA Modules:
  0.0 51.2 jit_solution(6308252948556697020)
XLA Ops:
  0.6 49.6 %shard_map.129 = (f32[2,16,32,256]{3,2,1,0:T(8,128)S(1)}, f32[2,16,8,128]{3,2,1,0:T(8,128)S(1)}, f32[16,8,128]{2,1,0:T(8,128)S(1)}) custom-call(s32[3,16]{1,0:T(4,128)} %group_in.1, f32[2,16,32,256]{3,2,1,0:T(8,128)} %noise_in.1, f32[16,32,256]{2,1,0:T(8,128)} %spec_in.1, bf16[2,256,256]{2,1,0:T(8,128)(2,1)} %constant.14.clone.za_in, ...), custom_call_target="tpu_custom_call" | custom-call | tf_op jit(solution)/shard_map/pallas_call | solution.py:525
  50.2 1.0 %shard_map.130 = (f32[2,16,32,256]{3,2,1,0:T(8,128)}, f32[2,8,16,128]{3,2,1,0:T(8,128)}, f32[2,4,8,64]{3,2,1,0:T(8,128)}, f32[2,2,4,32]{3,2,1,0:T(4,128)}) custom-call(f32[2,16,32,256]{3,2,1,0:T(8,128)S(1)} %get-tuple-element.7.mod_in, f32[2,16,8,128]{3,2,1,0:T(8,128)S(1)} %get-tuple-element.8.one_in, f32[16,8,128]{2,1,0:T(8,128)S(1)} %get-tuple-element.9.rest_in), custom_call_target="tpu_custom_call" | custom-call | tf_op jit(solution)/shard_map/pallas_call | solution.py:543
